TPU v7x, 256 devices: a whole 4x4x8 slice. The times are simulated.
256 devices in a mesh: tm: 32 (over z, y_lo, core), mom: 8 (over x, y_hi).
Axes of the slice: x: 4, y: 4 (y_hi: 2, y_lo: 2; y = y_hi * 2 + y_lo), z: 8, core: 2. Of those that a mesh axis runs over, the one named last changes fastest.
Arguments:
- sink_solutions: bfloat16 [32, 2, 512, 512], P('tm'), may hold values from -0.44921875 to 0.44921875
- noise_sources: bfloat16 [32, 2, 512, 512], P('tm'), may hold values from -0.44921875 to 0.44921875
- elementals: bfloat16 [8, 32, 2, 128, 128], P('mom', 'tm'), may hold values from -0.375 to 0.375
- pairs: int32 [8, 2], P('mom'), may hold values from 0 to 7
Outputs:
- blocks: bfloat16 [32, 4, 8, 2, 512, 512], P('tm', None, 'mom')
Inputs may be any that keep to these rules, and one draw needn't show every extreme that they name: `pairs`: entries are operator indices.
All inputs are finite; a program needn't handle non-finite values.
Results may differ from a plain program's by a relative error of at most 0.007.
Values may be sent and summed in bfloat16 or wider, within the bound.
No kernel may reach another device: no remote copies, remote signals or barrier semaphores. Data moves between devices by JAX's collectives and lax.ppermute only.
A program may use at most 64 MiB of HBM per device.

v0:
```python
import jax
import jax.numpy as jnp
from jax import lax
from jax.sharding import PartitionSpec as P

NSEP = 4


def laid_out(parts, dim):
    parts = jnp.moveaxis(parts, 0, dim)
    shape = parts.shape
    return parts.reshape(*shape[:dim], shape[dim] * shape[dim + 1], *shape[dim + 2 :])


def sent_to_all(x, axis):
    devices = lax.axis_size(axis)
    return lax.all_to_all(jnp.broadcast_to(x[None], (devices, *x.shape)), axis, 0, 0, tiled=True)


def gather_directly(x, axis, dim):
    return laid_out(sent_to_all(x, axis), dim)


def shifted(block, axis, distance):
    devices = range(lax.axis_size(axis))
    route = [((i - distance) % len(devices), i) for i in devices]
    return lax.ppermute(block, axis, route)


def transpose_product(left_mat, right_mat):
    return lax.dot_general(
        left_mat, right_mat, (((1,), (1,)), ((), ())), preferred_element_type=jnp.float32
    )


def complex_product(left_mat, right_mat):
    real_part = jnp.dot(left_mat[0], right_mat[0], preferred_element_type=jnp.float32) - jnp.dot(
        left_mat[1], right_mat[1], preferred_element_type=jnp.float32
    )
    imag_part = jnp.dot(left_mat[0], right_mat[1], preferred_element_type=jnp.float32) + jnp.dot(
        left_mat[1], right_mat[0], preferred_element_type=jnp.float32
    )
    return jnp.stack([real_part, imag_part])


def meson_function(sink_piece, noise_part, elemental):
    dilution_rows = sink_piece.shape[1]
    total_width = sink_piece.shape[2]
    eigenvector_count = elemental.shape[1]
    spinor_rows = sink_piece.reshape(
        2, dilution_rows * (total_width // eigenvector_count), eigenvector_count
    )
    applied_real = transpose_product(spinor_rows[0], elemental[0]) - transpose_product(
        spinor_rows[1], elemental[1]
    )
    applied_imaginary = transpose_product(spinor_rows[0], elemental[1]) + transpose_product(
        spinor_rows[1], elemental[0]
    )
    applied_result = (
        jnp.stack([applied_real, applied_imaginary])
        .reshape(2, dilution_rows, total_width)
        .astype(jnp.bfloat16)
    )
    meson_re = transpose_product(noise_part[0], applied_result[0]) + transpose_product(
        noise_part[1], applied_result[1]
    )
    meson_im = transpose_product(noise_part[0], applied_result[1]) - transpose_product(
        noise_part[1], applied_result[0]
    )
    return jnp.stack([meson_re, meson_im]).astype(jnp.bfloat16)


def local(sink_solutions, noise_sources, elementals, pairs):
    sink_piece = sink_solutions[0]
    noise_part = noise_sources[0]
    operator_sink = pairs[0, 0]
    operator_source = pairs[0, 1]
    held_elementals = elementals[:, 0]
    zeros_elemental = jnp.zeros_like(held_elementals[0])
    carried = (zeros_elemental, zeros_elemental)
    fragment = gather_directly(held_elementals, "mom", 0)
    row_count = fragment.shape[0]
    selected = []
    for position, wanted in enumerate((operator_sink, operator_source)):
        inside = (wanted >= 0) & (wanted < row_count)
        candidate = lax.dynamic_index_in_dim(
            fragment, jnp.clip(wanted, 0, row_count - 1), 0, keepdims=False
        )
        selected.append(jnp.where(inside, candidate, carried[position]))
    sink_elemental, source_elemental = tuple(selected)
    later_meson = meson_function(sink_piece, noise_part, sink_elemental)
    source_meson = meson_function(sink_piece, noise_part, source_elemental)
    arrived = []
    current_meson = later_meson
    for separation in range(NSEP):
        current_meson = shifted(current_meson, "tm", -1)
        arrived.append(current_meson)
    results = jnp.stack(
        [complex_product(moved_meson, source_meson).astype(jnp.bfloat16) for moved_meson in arrived]
    )
    return results[None, :, None]


def solution(mesh):
    return jax.shard_map(
        local,
        mesh=mesh,
        in_specs=(
            P("tm", None, None, None),
            P("tm", None, None, None),
            P("mom", "tm", None, None, None),
            P("mom", None),
        ),
        out_specs=P("tm", None, "mom", None, None, None),
        check_vma=False,
    )
```

profile of v0, /device:TPU:105, one launch (start us, length us, event | category | flops | bytes accessed | tf_op | source)
XLA Modules:
  0.0 107.8 jit_solution(17474587314325419651)
XLA Ops:
  0.0 1.7 %broadcast_in_dim.14 = bf16[8,1,2,128,128]{4,3,2,1,0:T(8,128)(2,1)} broadcast(bf16[2,128,128]{2,1,0:T(8,128)(2,1)} %bitcast.143), dimensions={2,3,4} | broadcast | bytes 589824 | tf_op jit(solution)/shard_map/broadcast_in_dim | solution.py:17
  1.7 5.8 %all-to-all-start = ((bf16[8,1,2,128,128]{4,3,2,1,0:T(8,128)(2,1)}), bf16[8,1,2,128,128]{4,3,2,1,0:T(8,128)(2,1)S(1)}, u32[]{:S(2)}, u32[]{:S(2)}) async-start(bf16[8,1,2,128,128]{4,3,2,1,0:T(8,128)(2,1)} %broadcast_in_dim.14), calls=%async_computation | async-start | bytes 1048576 | tf_op jit(solution)/shard_map/all_to_all | solution.py:17
  7.5 1.4 %fusion.63 = (s32[1,1]{1,0:T(1,128)}, s32[1,1]{1,0:T(1,128)}) fusion(s32[1,2]{1,0:T(1,128)} %param.7), kind=kLoop, calls=%fused_computation.95 | loop fusion | bytes 16 | tf_op jit(solution)/shard_map/slice | solution.py:76
  12.6 1.3 %fusion.62 = (bf16[1,1,512,512]{3,2,1,0:T(8,128)(2,1)S(1)}, bf16[1,1,512,512]{3,2,1,0:T(8,128)(2,1)S(1)}) fusion(bf16[1,2,512,512]{3,2,1,0:T(8,128)(2,1)} %param.4), kind=kLoop, calls=%fused_computation.94 | loop fusion | bytes 2097152 | tf_op jit(solution)/shard_map/slice | solution.py:54
  14.6 3.1 %all-to-all-done = bf16[8,1,2,128,128]{4,3,2,1,0:T(8,128)(2,1)S(1)} async-done(((bf16[8,1,2,128,128]{4,3,2,1,0:T(8,128)(2,1)}), bf16[8,1,2,128,128]{4,3,2,1,0:T(8,128)(2,1)S(1)}, u32[]{:S(2)}, u32[]{:S(2)}) %all-to-all-start) | async-done | bytes 524320 | tf_op jit(solution)/shard_map/all_to_all | solution.py:17
  17.7 1.3 %fusion.59 = f32[128,2048]{1,0:T(8,128)} fusion(bf16[2048,128]{1,0:T(8,128)(2,1)S(1)} %squeeze.44, bf16[1,1,2,128,128]{4,3,2,1,0:T(8,128)(2,1)S(1)} %get-tuple-element.7), kind=kOutput, calls=%fused_computation.91 | convolution fusion | flops 67108864 | bytes 1605632 | tf_op jit(solution)/shard_map/dot_general | solution.py:31
  19.0 1.3 %fusion.58 = f32[128,2048]{1,0:T(8,128)} fusion(bf16[2048,128]{1,0:T(8,128)(2,1)S(1)} %squeeze.44, bf16[1,1,2,128,128]{4,3,2,1,0:T(8,128)(2,1)S(1)} %get-tuple-element.7), kind=kOutput, calls=%fused_computation.90 | convolution fusion | flops 67108864 | bytes 1605632 | tf_op jit(solution)/shard_map/dot_general | solution.py:31
  21.5 1.6 %fusion.6 = bf16[2048,128]{0,1:T(8,128)(2,1)S(1)} fusion(f32[128,2048]{1,0:T(8,128)} %fusion.59, bf16[2048,128]{1,0:T(8,128)(2,1)S(1)} %squeeze.46, bf16[1,1,2,128,128]{4,3,2,1,0:T(8,128)(2,1)S(1)} %get-tuple-element.7), kind=kOutput, calls=%fused_computation.11 | convolution fusion | flops 67633152 | bytes 2129920 | tf_op jit(solution)/shard_map/dot_general | solution.py:31
  23.1 1.0 copy.7
  24.1 1.4 %squeeze.49 = bf16[512,512]{1,0:T(8,128)(2,1)S(1)} reshape(bf16[2048,128]{1,0:T(8,128)(2,1)} %copy.7) | data formatting | bytes 1048576 | tf_op jit(solution)/shard_map/squeeze | solution.py:65
  25.5 2.3 %fusion.7 = bf16[2048,128]{0,1:T(8,128)(2,1)} fusion(f32[128,2048]{1,0:T(8,128)} %fusion.58, bf16[2048,128]{1,0:T(8,128)(2,1)S(1)} %squeeze.46, bf16[1,1,2,128,128]{4,3,2,1,0:T(8,128)(2,1)S(1)} %get-tuple-element.7), kind=kOutput, calls=%fused_computation.12 | convolution fusion | flops 67633152 | bytes 2129920 | tf_op jit(solution)/shard_map/dot_general | solution.py:31
  27.8 2.0 %copy.6 = bf16[2048,128]{1,0:T(8,128)(2,1)} copy(bf16[2048,128]{0,1:T(8,128)(2,1)} %fusion.7) | data formatting | bytes 1048576 | tf_op jit(solution)/shard_map/sub | solution.py:53
  29.8 2.1 %squeeze.47 = bf16[512,512]{1,0:T(8,128)(2,1)} reshape(bf16[2048,128]{1,0:T(8,128)(2,1)} %copy.6) | data formatting | bytes 1048576 | tf_op jit(solution)/shard_map/squeeze | solution.py:64
  32.0 1.6 %fusion.40 = f32[512,512]{1,0:T(8,128)S(1)} fusion(bf16[512,512]{1,0:T(8,128)(2,1)} %squeeze.47, bf16[1,2,512,512]{3,2,1,0:T(8,128)(2,1)S(1)} %copy-done), kind=kOutput, calls=%fused_computation.66 | convolution fusion | flops 268435456 | bytes 2097152 | tf_op jit(solution)/shard_map/dot_general | solution.py:31
  35.0 1.1 pad_maximum_fusion
  36.1 1.6 %collective-permute-start = (bf16[2,512,512]{1,2,0:T(8,128)(2,1)}, bf16[2,512,512]{1,2,0:T(8,128)(2,1)}, u32[]{:S(2)}, u32[]{:S(2)}) collective-permute-start(bf16[2,512,512]{1,2,0:T(8,128)(2,1)} %pad_maximum_fusion), channel_id=1, source_target_pairs={{8,0},{16,8},{24,16},{32,24},{40,32},{48,40},{56,48},{64,56},{72,6... | collective-permute-start | bytes 3145736 | tf_op jit(solution)/shard_map/ppermute | solution.py:27
  39.9 14.2 %collective-permute-done = bf16[2,512,512]{1,2,0:T(8,128)(2,1)} collective-permute-done((bf16[2,512,512]{1,2,0:T(8,128)(2,1)}, bf16[2,512,512]{1,2,0:T(8,128)(2,1)}, u32[]{:S(2)}, u32[]{:S(2)}) %collective-permute-start) | collective-permute-done | bytes 1048608 | tf_op jit(solution)/shard_map/ppermute | solution.py:27
  55.0 1.5 %fusion.42 = f32[512,512]{1,0:T(8,128)S(1)} fusion(bf16[512,512]{1,0:T(8,128)(2,1)S(1)} %fusion.10, bf16[2,512,512]{1,2,0:T(8,128)(2,1)} %collective-permute-done), kind=kOutput, calls=%fused_computation.68 | convolution fusion | flops 268435456 | bytes 2097152 | tf_op jit(solution)/shard_map/dot_general | solution.py:40
  56.5 1.5 %fusion.43 = f32[512,512]{1,0:T(8,128)S(1)} fusion(bf16[512,512]{1,0:T(8,128)(2,1)S(1)} %fusion.12, bf16[2,512,512]{1,2,0:T(8,128)(2,1)} %collective-permute-done), kind=kOutput, calls=%fused_computation.69 | convolution fusion | flops 268435456 | bytes 2097152 | tf_op jit(solution)/shard_map/dot_general | solution.py:37
  58.0 12.5 %collective-permute-done.1 = bf16[2,512,512]{1,2,0:T(8,128)(2,1)S(1)} collective-permute-done((bf16[2,512,512]{1,2,0:T(8,128)(2,1)}, bf16[2,512,512]{1,2,0:T(8,128)(2,1)S(1)}, u32[]{:S(2)}, u32[]{:S(2)}) %collective-permute-start.1) | collective-permute-done | bytes 1048608 | tf_op jit(solution)/shard_map/ppermute | solution.py:27
  70.6 1.5 %fusion.26 = bf16[1,1,512,512]{3,2,1,0:T(8,128)(2,1)S(1)} fusion(f32[512,512]{1,0:T(8,128)S(1)} %fusion.42, bf16[512,512]{1,0:T(8,128)(2,1)S(1)} %fusion.12, bf16[2,512,512]{1,2,0:T(8,128)(2,1)} %collective-permute-done), kind=kOutput, calls=%fused_computation.43 | convolution fusion | flops 268959744 | bytes 2621440 | tf_op jit(solution)/shard_map/dot_general | solution.py:40
  72.1 1.5 %fusion.27 = bf16[1,1,512,512]{3,2,1,0:T(8,128)(2,1)S(1)} fusion(f32[512,512]{1,0:T(8,128)S(1)} %fusion.43, bf16[512,512]{1,0:T(8,128)(2,1)S(1)} %fusion.10, bf16[2,512,512]{1,2,0:T(8,128)(2,1)} %collective-permute-done), kind=kOutput, calls=%fused_computation.44 | convolution fusion | flops 268959744 | bytes 2621440 | tf_op jit(solution)/shard_map/dot_general | solution.py:37
  74.1 0.5 fusion.24
  75.1 11.8 %collective-permute-done.2 = bf16[2,512,512]{1,2,0:T(8,128)(2,1)S(1)} collective-permute-done((bf16[2,512,512]{1,2,0:T(8,128)(2,1)S(1)}, bf16[2,512,512]{1,2,0:T(8,128)(2,1)S(1)}, u32[]{:S(2)}, u32[]{:S(2)}) %collective-permute-start.2) | collective-permute-done | bytes 1048608 | tf_op jit(solution)/shard_map/ppermute | solution.py:27
  87.4 0.5 fusion.46
  87.9 0.5 fusion.22
  88.9 0.5 fusion.23
  89.3 13.9 %collective-permute-done.3 = bf16[2,512,512]{1,2,0:T(8,128)(2,1)S(1)} collective-permute-done((bf16[2,512,512]{1,2,0:T(8,128)(2,1)S(1)}, bf16[2,512,512]{1,2,0:T(8,128)(2,1)S(1)}, u32[]{:S(2)}, u32[]{:S(2)}) %collective-permute-start.3) | collective-permute-done | bytes 1048608 | tf_op jit(solution)/shard_map/ppermute | solution.py:27
  103.2 0.5 fusion.48
  104.2 0.5 fusion.20
  104.7 0.5 fusion.21
  105.2 2.6 %maximum_bitcast_fusion = bf16[1,4,1,2,512,512]{5,4,3,2,1,0:T(8,128)(2,1)} fusion(bf16[1,1,512,512]{3,2,1,0:T(8,128)(2,1)S(1)} %fusion.20, bf16[1,1,512,512]{3,2,1,0:T(8,128)(2,1)S(1)} %fusion.21, bf16[1,1,512,512]{3,2,1,0:T(8,128)(2,1)S(1)} %fusion.22, bf16[1,1,512,512]{3,2,1,0:T(8,128)(2,1)S(1)} %fusion.23, bf16[1,1,512,512]{3,2,1,0:T(8,128)(2,1)S(1)} %fusion.24, ...), kind=kLoop, calls=%fused_computation | loop fusion | flops 14680064 | bytes 8388608 | tf_op jit(solution)/shard_map/broadcast_in_dim | solution.py:101
  (30 shorter events, 8.7 us)
Async XLA Ops:
  1.7 16.0 %all-to-all-start = ((bf16[8,1,2,128,128]{4,3,2,1,0:T(8,128)(2,1)}), bf16[8,1,2,128,128]{4,3,2,1,0:T(8,128)(2,1)S(1)}, u32[]{:S(2)}, u32[]{:S(2)}) async-start(bf16[8,1,2,128,128]{4,3,2,1,0:T(8,128)(2,1)} %broadcast_in_dim.14), calls=%async_computation | async-start | bytes 1048576 | tf_op jit(solution)/shard_map/all_to_all | solution.py:17
  21.5 10.5 %copy-start = (bf16[1,2,512,512]{3,2,1,0:T(8,128)(2,1)S(1)}, bf16[1,2,512,512]{3,2,1,0:T(8,128)(2,1)}, u32[]{:S(2)}) copy-start(bf16[1,2,512,512]{3,2,1,0:T(8,128)(2,1)} %param.5) | copy-start | bytes 3145732
  32.0 2.5 %copy-start.1 = (bf16[512,512]{1,0:T(8,128)(2,1)S(1)}, bf16[512,512]{1,0:T(8,128)(2,1)}, u32[]{:S(2)}) copy-start(bf16[512,512]{1,0:T(8,128)(2,1)} %squeeze.47) | copy-start | bytes 1572868
  36.1 17.9 %collective-permute-start = (bf16[2,512,512]{1,2,0:T(8,128)(2,1)}, bf16[2,512,512]{1,2,0:T(8,128)(2,1)}, u32[]{:S(2)}, u32[]{:S(2)}) collective-permute-start(bf16[2,512,512]{1,2,0:T(8,128)(2,1)} %pad_maximum_fusion), channel_id=1, source_target_pairs={{8,0},{16,8},{24,16},{32,24},{40,32},{48,40},{56,48},{64,56},{72,6... | collective-permute-start | bytes 3145736 | tf_op jit(solution)/shard_map/ppermute | solution.py:27
  54.0 16.5 %collective-permute-start.1 = (bf16[2,512,512]{1,2,0:T(8,128)(2,1)}, bf16[2,512,512]{1,2,0:T(8,128)(2,1)S(1)}, u32[]{:S(2)}, u32[]{:S(2)}) collective-permute-start(bf16[2,512,512]{1,2,0:T(8,128)(2,1)} %collective-permute-done), channel_id=1, source_target_pairs={{8,0},{16,8},{24,16},{32,24},{40,32},{48,40},{56,48},{64,56},{72,6... | collective-permute-start | bytes 3145736 | tf_op jit(solution)/shard_map/ppermute | solution.py:27
  70.6 16.3 %collective-permute-start.2 = (bf16[2,512,512]{1,2,0:T(8,128)(2,1)S(1)}, bf16[2,512,512]{1,2,0:T(8,128)(2,1)S(1)}, u32[]{:S(2)}, u32[]{:S(2)}) collective-permute-start(bf16[2,512,512]{1,2,0:T(8,128)(2,1)S(1)} %collective-permute-done.1), channel_id=1, source_target_pairs={{8,0},{16,8},{24,16},{32,24},{40,32},{48,40},{56,48},{64,56},{72,6... | collective-permute-start | bytes 3145736 | tf_op jit(solution)/shard_map/ppermute | solution.py:27
  86.9 16.3 %collective-permute-start.3 = (bf16[2,512,512]{1,2,0:T(8,128)(2,1)S(1)}, bf16[2,512,512]{1,2,0:T(8,128)(2,1)S(1)}, u32[]{:S(2)}, u32[]{:S(2)}) collective-permute-start(bf16[2,512,512]{1,2,0:T(8,128)(2,1)S(1)} %collective-permute-done.2), channel_id=1, source_target_pairs={{8,0},{16,8},{24,16},{32,24},{40,32},{48,40},{56,48},{64,56},{72,6... | collective-permute-start | bytes 3145736 | tf_op jit(solution)/shard_map/ppermute | solution.py:27
where the time goes:
time: 109 us; the launch traced here: 108 us
  waiting for transfers between devices  55.5 us (51%)
  matrix products  24.4 us (22%)
  local copies, waits for them, and re-layouts  12.7 us (12%)
  starting transfers between devices  7.39 us (7%)
  between operations  4.03 us (4%)
  other arithmetic  3.69 us (3%)
    ppermute x4, waiting for transfers between devices, shifted(): return lax.ppermute(block, axis, route)  52.4 us
    dot_general x16, matrix products, transpose_product(): lax.dot_general(left_mat, right_mat, (((1,), (1,)), ((), ())), preferred_...  12.5 us
    all_to_all x1, starting transfers between devices, sent_to_all(): lax.all_to_all(jnp.broadcast_to(x[None], (devices, *x.shape)), axis, 0, 0...  5.75 us
    all_to_all x1, waiting for transfers between devices, sent_to_all(): lax.all_to_all(jnp.broadcast_to(x[None], (devices, *x.shape)), axis, 0, 0...  3.13 us
    dot_general x4, matrix products, complex_product(): jnp.dot(left_mat[0], right_mat[0], preferred_element_type=jnp.float32)  2.99 us
    dot_general x4, matrix products, complex_product(): jnp.dot(left_mat[0], right_mat[1], preferred_element_type=jnp.float32)  2.99 us
    dot_general x4, matrix products, complex_product(): jnp.dot(left_mat[1], right_mat[0], preferred_element_type=jnp.float32)  2.98 us
    dot_general x4, matrix products, complex_product(): jnp.dot(left_mat[1], right_mat[1], preferred_element_type=jnp.float32)  2.98 us
  transfers between devices with their start and end apart: 5, of which 5 were waited for; matrix products, arithmetic and copies ran while one was open for 15% of the time, Pallas kernels for 0%

commit v1 on v0

v1 whole, which is shorter than its diff:
```python
import functools

import jax
import jax.numpy as jnp
from jax import lax
from jax.experimental import pallas as pl
from jax.experimental.pallas import tpu as pltpu
from jax.sharding import PartitionSpec as P


NSEP = 4
VMEM_LIMIT = 24 * 1024 * 1024
F32 = jnp.float32
BF16 = jnp.bfloat16
VMEM, SMEM, HBM = pltpu.VMEM, pltpu.SMEM, pltpu.HBM
DMA = pltpu.SemaphoreType.DMA


def transpose_product(left_mat, right_mat):
    return lax.dot_general(
        left_mat, right_mat, (((1,), (1,)), ((), ())), preferred_element_type=F32
    )


def in_space(space, count=1):
    return [pl.BlockSpec(memory_space=space)] * count


def fixed(array, space):
    return pltpu.with_memory_space_constraint(array, space)


def kernel_call(body, flops, in_specs, out_shape, scratch=(), **options):
    many = isinstance(out_shape, list)
    spaces = [in_space(shape.memory_space)[0] for shape in (out_shape if many else [out_shape])]
    return pl.pallas_call(
        body,
        in_specs=in_specs,
        out_specs=spaces if many else spaces[0],
        out_shape=out_shape,
        scratch_shapes=scratch,
        compiler_params=pltpu.CompilerParams(vmem_limit_bytes=VMEM_LIMIT),
        cost_estimate=pl.CostEstimate(flops=flops, bytes_accessed=3_000_000, transcendentals=0),
        **options,
    )


def outgoing_kernel(mom_ref, time_ref, phi_hbm, rho_hbm, piece_ref, sems):
    del time_ref
    nev = piece_ref.shape[2]
    cols = pl.ds(pl.multiple_of(mom_ref[0] // 2 * nev, nev), nev)
    copies = [
        pltpu.make_async_copy(
            source.at[0, part, :, cols], piece_ref.at[2 * which + part], sems.at[2 * which + part]
        )
        for which, source in enumerate((phi_hbm, rho_hbm))
        for part in range(2)
    ]
    for copy in copies:
        copy.start()
    for copy in copies:
        copy.wait()


def outgoing(mom, time, sink, noise, nev):
    rows = sink.shape[2]
    return kernel_call(
        outgoing_kernel,
        1_000_000,
        in_space(SMEM, 2) + in_space(HBM, 2),
        VMEM((4, rows, nev), BF16),
        [DMA((4,))],
    )(mom, time, fixed(sink, HBM), fixed(noise, HBM))


def stage_kernel(phi_hbm, rho_hbm, phi, rho, sems):
    spins, nev = phi.shape[0], phi.shape[2] // 2
    copies = []
    for source, held in ((phi_hbm, phi), (rho_hbm, rho)):
        for spin in range(spins):
            for part in range(2):
                copies.append(
                    pltpu.make_async_copy(
                        source.at[0, part, :, pl.ds(spin * nev, nev)],
                        held.at[spin, :, pl.ds(part * nev, nev)],
                        sems.at[len(copies)],
                    )
                )
                copies[-1].start()
    for copy in copies:
        copy.wait()


def stage(sink, noise, nev):
    rows, width = sink.shape[2:]
    spins = width // nev
    return kernel_call(
        stage_kernel,
        1_000_000,
        in_space(HBM, 2),
        [VMEM((spins, rows, 2 * nev), BF16)] * 2,
        [DMA((4 * spins,))],
    )(fixed(sink, HBM), fixed(noise, HBM))


def fill_weights(elem, weights):
    nev = elem.shape[1]
    re, im = elem[0], elem[1]
    weights[:nev, :nev], weights[:nev, nev:] = re, -im
    weights[nev:, :nev], weights[nev:, nev:] = im, re


def apply_elemental(phi, weights, right, at):
    nev = phi.shape[1] // 2
    applied = transpose_product(weights, phi).astype(BF16)
    right[0, at : at + 2 * nev] = applied
    right[1, at : at + nev] = applied[nev:]
    right[1, at + nev : at + 2 * nev] = -applied[:nev]


def plain_product(left, right):
    return jnp.dot(left, right, preferred_element_type=F32)


def own_meson_kernel(which, columns, pairs_ref, mom_ref, phi, rho, own_hbm, *refs):
    *others, out_ref, chosen, weights, right, sem = refs
    spins, nev = phi.shape[0], phi.shape[2] // 2
    own_copy = pltpu.make_async_copy(own_hbm.at[0, 0], chosen, sem)
    own_copy.start()
    wanted, mom = pairs_ref[0, which], mom_ref[0]
    distance = lax.rem(mom // 2 - wanted // 2 + columns, columns)
    slot = distance + columns * lax.rem(wanted + mom, 2)
    own_copy.wait()
    for index, other in enumerate(others):
        @pl.when(slot == index + 1)
        def _():
            chosen[...] = other[...]

    fill_weights(chosen, weights)
    for spin in range(spins):
        apply_elemental(phi[spin], weights[...], right, spin * 2 * nev)
    left = jnp.concatenate([rho[spin] for spin in range(spins)], axis=1)
    for part in range(2):
        out_ref[part] = plain_product(left, right[part]).astype(BF16)


def own_meson(which, pairs, mom, phi, rho, elementals, others):
    spins, rows, nev = phi.shape[0], phi.shape[1], phi.shape[2] // 2
    return kernel_call(
        functools.partial(own_meson_kernel, which, (len(others) + 1) // 2),
        1_340_000_000,
        in_space(SMEM, 2) + in_space(VMEM, 2) + in_space(HBM) + in_space(VMEM, len(others)),
        [VMEM((2, rows, rows), BF16), VMEM((2, nev, nev), BF16)],
        [VMEM((2 * nev, 2 * nev), BF16), VMEM((2, spins * 2 * nev, rows), BF16), DMA],
    )(fixed(pairs, HBM), mom, phi, rho, fixed(elementals, HBM), *others)


def pieces_kernel(count, *refs):
    pieces, elem_ref = refs[:count], refs[count]
    before = refs[count + 1 : -3]
    out_ref, weights, right = refs[-3:]
    nev = elem_ref.shape[1]
    fill_weights(elem_ref, weights)
    for index, piece in enumerate(pieces):
        phi = jnp.concatenate([piece[0], piece[1]], axis=1)
        apply_elemental(phi, weights[...], right, index * 2 * nev)
    left = jnp.concatenate([piece[part] for piece in pieces for part in (2, 3)], axis=1)
    for part in range(2):
        term = plain_product(left, right[part])
        out_ref[part] = (term + before[0][part] if before else term).astype(out_ref.dtype)


def meson_of_pieces(pieces, elemental, before, kind):
    rows, nev = pieces[0].shape[1:]
    operands = [*pieces, elemental, *before]
    return kernel_call(
        functools.partial(pieces_kernel, len(pieces)),
        340_000_000 * len(pieces),
        in_space(VMEM, len(operands)),
        VMEM((2, rows, rows), kind),
        [VMEM((2 * nev, 2 * nev), BF16), VMEM((2, 2 * nev * len(pieces), rows), BF16)],
    )(*operands)


def product_kernel(place, choices, time_ref, *refs):
    lefts, right = refs[:choices], refs[choices]
    out_hbm, held, sems = refs[-3:]
    core = lax.rem(time_ref[0], 2)
    rows = right.shape[1]
    half = rows // 2
    copies = []
    for step in range(2):
        lines = pl.ds(step * half, half)
        left = [ref[:, lines] for ref in lefts]
        left = left[0] if choices == 1 else jnp.where(core == 0, *left)
        for part in range(2):
            if part == 0:
                term = plain_product(left[0], right[0]) - plain_product(left[1], right[1])
            else:
                term = plain_product(left[0], right[1]) + plain_product(left[1], right[0])
            held[part, lines] = term.astype(BF16)
            copies.append(
                pltpu.make_async_copy(
                    held.at[part, lines], out_hbm.at[0, place(core), 0, part, lines], sems.at[len(copies)]
                )
            )
            copies[-1].start()
    for copy in copies:
        copy.wait()


def product(place, time, lefts, right, blocks):
    rows = right.shape[2]
    operands = [time, *lefts, right] + ([] if blocks is None else [blocks])
    return kernel_call(
        functools.partial(product_kernel, place, len(lefts)),
        1_080_000_000,
        in_space(SMEM)
        + in_space(VMEM, len(lefts) + 1)
        + ([] if blocks is None else in_space(pl.ANY)),
        HBM((1, NSEP, 1, 2, rows, rows), BF16),
        [VMEM((2, rows, rows), BF16), DMA((4,))],
        input_output_aliases={} if blocks is None else {len(operands) - 1: 0},
    )(*operands)


def local(sink, noise, elementals, pairs):
    times, moms = lax.axis_size("tm"), lax.axis_size("mom")
    nev = elementals.shape[3]
    columns = moms // 2
    mom, time = lax.axis_index("mom").reshape(1), lax.axis_index("tm").reshape(1)

    def earlier(block, distance):
        return lax.ppermute(block, "tm", [(t, (t - distance) % times) for t in range(times)])

    def partner(block, keep=lambda t: True):
        return lax.ppermute(block, "tm", [(t, t ^ 1) for t in range(times) if keep(t)])

    def along_x(block, distance):
        route = [(m, (m // 2 + distance) % columns * 2 + m % 2) for m in range(moms)]
        return lax.ppermute(block, "mom", route)

    own = elementals[0, 0]
    across = lax.ppermute(own, "mom", [(m, m ^ 1) for m in range(moms)])
    piece = outgoing(mom, time, sink, noise, nev)
    piece = earlier(piece, 4)
    near, far = {}, {0: across}
    for distance in (1, 3, 2):
        near[distance] = along_x(own, distance)
    for distance in (1, 3, 2):
        far[distance] = along_x(across, distance)
    others = [near[d] for d in range(1, columns)] + [far[d] for d in range(columns)]

    phi, rho = stage(sink, noise, nev)

    def meson(which):
        return own_meson(which, pairs, mom, phi, rho, elementals, others)

    sink_meson, sink_elemental = meson(0)
    later_elemental = earlier(sink_elemental, 4)
    two_later = earlier(sink_meson, 2)
    pieces = {0: piece}
    for distance in (1, 3, 2):
        pieces[distance] = along_x(piece, distance)
    beside = partner(sink_meson, lambda t: t % 2 == 1)
    source_meson, _ = meson(1)

    partial_sum = meson_of_pieces([pieces[d] for d in (0, 1, 3)], later_elemental, [], F32)
    four_later = meson_of_pieces([pieces[2]], later_elemental, [partial_sum], BF16)
    beside_four = partner(four_later, lambda t: t % 2 == 0)
    beside_two = partner(two_later)

    blocks = product(lambda c: 1, time, [two_later], source_meson, None)
    blocks = product(lambda c: 3, time, [four_later], source_meson, blocks)
    blocks = product(lambda c: 2 - 2 * c, time, [beside_two], source_meson, blocks)
    return product(lambda c: 2 * c, time, [beside, beside_four], source_meson, blocks)


def solution(mesh):
    return jax.shard_map(
        local,
        mesh=mesh,
        in_specs=(
            P("tm", None, None, None),
            P("tm", None, None, None),
            P("mom", "tm", None, None, None),
            P("mom", None),
        ),
        out_specs=P("tm", None, "mom", None, None, None),
        check_vma=False,
    )
```

time: 109 us -> 94.5 us (0.87)
  the two profiles are of different devices: /device:TPU:105 before, /device:TPU:22 now
where the time goes in v1:
time: 94.5 us; the launch traced here: 94.2 us
  waiting for transfers between devices  49.4 us (52%)
  starting transfers between devices  25.4 us (27%)
  Pallas kernels  19.1 us (20%)
    ppermute x3, waiting for transfers between devices, earlier(): lax.ppermute(block, 'tm', [(t, (t - distance) % times) for t in range(tim...  31.7 us
    ppermute x9, waiting for transfers between devices, along_x(): return lax.ppermute(block, 'mom', route)  15.1 us
    ppermute x3, starting transfers between devices, earlier(): lax.ppermute(block, 'tm', [(t, (t - distance) % times) for t in range(tim...  11.4 us
    ppermute x9, starting transfers between devices, along_x(): return lax.ppermute(block, 'mom', route)  9.65 us
    pallas_call x4, Pallas kernels, product(): kernel_call(functools.partial(product_kernel, place, len(lefts)), 1080000...  8.08 us
    pallas_call x2, Pallas kernels, own_meson(): kernel_call(functools.partial(own_meson_kernel, which, (len(others) + 1)...  6.17 us
    ppermute x3, starting transfers between devices, partner(): lax.ppermute(block, 'tm', [(t, t ^ 1) for t in range(times) if keep(t)])  4.09 us
    ppermute x1, waiting for transfers between devices, local(): across = lax.ppermute(own, 'mom', [(m, m ^ 1) for m in range(moms)])  2.6 us
  transfers between devices with their start and end apart: 16, of which 7 were waited for; matrix products, arithmetic and copies ran while one was open for 0% of the time, Pallas kernels for 15%

profile of v1, /device:TPU:22, one launch (start us, length us, event | category | flops | bytes accessed | tf_op | source)
XLA Modules:
  0.0 94.2 jit_solution(641130775102804923)
XLA Ops:
  0.0 0.3 collective-permute-start.3
  0.3 2.2 %collective-permute-start = (bf16[2,128,128]{2,1,0:T(8,128)(2,1)}, bf16[2,128,128]{2,1,0:T(8,128)(2,1)S(1)}, u32[]{:S(2)}, u32[]{:S(2)}) collective-permute-start(bf16[2,128,128]{2,1,0:T(8,128)(2,1)} %bitcast.4), channel_id=1, source_target_pairs={{0,2},{1,3},{2,4},{3,5},{4,6},{5,7},{6,0},{7,1},{8,10},{9,11},{10,... | collective-permute-start | bytes 196616 | tf_op jit(solution)/shard_map/ppermute | solution.py:241
  2.5 0.7 collective-permute-start.1
  3.2 0.1 collective-permute-start.2
  3.4 2.6 %collective-permute-done.3.refs_3_ = bf16[2,128,128]{2,1,0:T(8,128)(2,1)S(1)} collective-permute-done((bf16[2,128,128]{2,1,0:T(8,128)(2,1)}, bf16[2,128,128]{2,1,0:T(8,128)(2,1)S(1)}, u32[]{:S(2)}, u32[]{:S(2)}) %collective-permute-start.3) | collective-permute-done | bytes 65568 | tf_op jit(solution)/shard_map/ppermute | solution.py:244
  6.0 0.5 collective-permute-start.4
  6.5 2.4 %collective-permute-start.5 = (bf16[2,128,128]{2,1,0:T(8,128)(2,1)S(1)}, bf16[2,128,128]{2,1,0:T(8,128)(2,1)S(1)}, u32[]{:S(2)}, u32[]{:S(2)}) collective-permute-start(bf16[2,128,128]{2,1,0:T(8,128)(2,1)S(1)} %collective-permute-done.3.refs_3_), channel_id=1, source_target_pairs={{0,4},{1,5},{2,6},{3,7},{4,0},{5,1},{6,2},{7,3},{8,12},{9,13},{10,... | collective-permute-start | bytes 196616 | tf_op jit(solution)/shard_map/ppermute | solution.py:241
  8.9 1.8 %shard_map.46 = (bf16[4,512,256]{2,1,0:T(8,128)(2,1)S(1)}, bf16[4,512,256]{2,1,0:T(8,128)(2,1)S(1)}) custom-call(bf16[1,2,512,512]{3,2,1,0:T(8,128)(2,1)} %phi_hbm.3, bf16[1,2,512,512]{3,2,1,0:T(8,128)(2,1)} %rho_hbm.3), custom_call_target="tpu_custom_call" | custom-call | flops 1000000 | bytes 3000000 | tf_op jit(solution)/shard_map/pallas_call | solution.py:97
  10.7 1.2 %shard_map.48 = bf16[4,512,128]{2,1,0:T(8,128)(2,1)S(1)} custom-call(s32[1]{0:T(128)} %bitcast.1.mom_ref, s32[1]{0:T(128)} %bitcast.time_ref, bf16[1,2,512,512]{3,2,1,0:T(8,128)(2,1)} %phi_hbm.3, bf16[1,2,512,512]{3,2,1,0:T(8,128)(2,1)} %rho_hbm.3), custom_call_target="tpu_custom_call" | custom-call | flops 1000000 | bytes 3000000 | tf_op jit(solution)/shard_map/pallas_call | solution.py:67
  11.9 0.4 collective-permute-done.5.refs_5_
  12.2 2.1 %collective-permute-done.6.refs_6_ = bf16[2,128,128]{2,1,0:T(8,128)(2,1)S(1)} collective-permute-done((bf16[2,128,128]{2,1,0:T(8,128)(2,1)S(1)}, bf16[2,128,128]{2,1,0:T(8,128)(2,1)S(1)}, u32[]{:S(2)}, u32[]{:S(2)}) %collective-permute-start.6) | collective-permute-done | bytes 65568 | tf_op jit(solution)/shard_map/ppermute | solution.py:241
  14.4 3.1 %shard_map.47 = (bf16[2,512,512]{2,1,0:T(8,128)(2,1)S(1)}, bf16[2,128,128]{2,1,0:T(8,128)(2,1)S(1)}) custom-call(s32[1,2]{1,0:T(1,128)} %pairs_ref.3, s32[1]{0:T(128)} %bitcast.1.mom_ref, bf16[4,512,256]{2,1,0:T(8,128)(2,1)S(1)} %get-tuple-element.10.phi, bf16[4,512,256]{2,1,0:T(8,128)(2,1)S(1)} %get-tuple-element.11.rho, ...), custom_call_target="tpu_custom_call" | custom-call | flops 1340000000 | bytes 3000000 | tf_op jit(solution)/shard_map/pallas_call | solution.py:149
  17.4 6.7 %collective-permute-start.14 = (bf16[2,512,512]{2,1,0:T(8,128)(2,1)S(1)}, bf16[2,512,512]{2,1,0:T(8,128)(2,1)S(1)}, u32[]{:S(2)}, u32[]{:S(2)}) collective-permute-start(bf16[2,512,512]{2,1,0:T(8,128)(2,1)S(1)} %get-tuple-element.12), channel_id=1, source_target_pairs={{0,240},{8,248},{16,0},{24,8},{32,16},{40,24},{48,32},{56,40},{64,... | collective-permute-start | bytes 3145736 | tf_op jit(solution)/shard_map/ppermute | solution.py:234
  24.1 1.0 %collective-permute-start.8 = (bf16[4,512,128]{2,1,0:T(8,128)(2,1)S(1)}, bf16[4,512,128]{2,1,0:T(8,128)(2,1)S(1)}, u32[]{:S(2)}, u32[]{:S(2)}) collective-permute-start(bf16[4,512,128]{2,1,0:T(8,128)(2,1)S(1)} %shard_map.48), channel_id=1, source_target_pairs={{0,224},{8,232},{16,240},{24,248},{32,0},{40,8},{48,16},{56,24},{6... | collective-permute-start | bytes 1572872 | tf_op jit(solution)/shard_map/ppermute | solution.py:234
  25.1 29.8 %collective-permute-done.8.refs_0_ = bf16[4,512,128]{2,1,0:T(8,128)(2,1)S(1)} collective-permute-done((bf16[4,512,128]{2,1,0:T(8,128)(2,1)S(1)}, bf16[4,512,128]{2,1,0:T(8,128)(2,1)S(1)}, u32[]{:S(2)}, u32[]{:S(2)}) %collective-permute-start.8) | collective-permute-done | bytes 524320 | tf_op jit(solution)/shard_map/ppermute | solution.py:234
  54.9 1.7 %collective-permute-start.11 = (bf16[4,512,128]{2,1,0:T(8,128)(2,1)S(1)}, bf16[4,512,128]{2,1,0:T(8,128)(2,1)S(1)}, u32[]{:S(2)}, u32[]{:S(2)}) collective-permute-start(bf16[4,512,128]{2,1,0:T(8,128)(2,1)S(1)} %collective-permute-done.8.refs_0_), channel_id=1, source_target_pairs={{0,2},{1,3},{2,4},{3,5},{4,6},{5,7},{6,0},{7,1},{8,10},{9,11},{10,... | collective-permute-start | bytes 1572872 | tf_op jit(solution)/shard_map/ppermute | solution.py:241
  56.5 0.4 collective-permute-start.12
  56.9 1.7 %collective-permute-start.9 = (bf16[4,512,128]{2,1,0:T(8,128)(2,1)S(1)}, bf16[4,512,128]{2,1,0:T(8,128)(2,1)S(1)}, u32[]{:S(2)}, u32[]{:S(2)}) collective-permute-start(bf16[4,512,128]{2,1,0:T(8,128)(2,1)S(1)} %collective-permute-done.8.refs_0_), channel_id=1, source_target_pairs={{0,4},{1,5},{2,6},{3,7},{4,0},{5,1},{6,2},{7,3},{8,12},{9,13},{10,... | collective-permute-start | bytes 1572872 | tf_op jit(solution)/shard_map/ppermute | solution.py:241
  58.6 3.7 %collective-permute-start.10 = (bf16[2,128,128]{2,1,0:T(8,128)(2,1)S(1)}, bf16[2,128,128]{2,1,0:T(8,128)(2,1)S(1)}, u32[]{:S(2)}, u32[]{:S(2)}) collective-permute-start(bf16[2,128,128]{2,1,0:T(8,128)(2,1)S(1)} %get-tuple-element.13), channel_id=1, source_target_pairs={{0,224},{8,232},{16,240},{24,248},{32,0},{40,8},{48,16},{56,24},{6... | collective-permute-start | bytes 196616 | tf_op jit(solution)/shard_map/ppermute | solution.py:234
  62.3 1.9 %collective-permute-done.10.refs_3_.refs_1_ = bf16[2,128,128]{2,1,0:T(8,128)(2,1)S(1)} collective-permute-done((bf16[2,128,128]{2,1,0:T(8,128)(2,1)S(1)}, bf16[2,128,128]{2,1,0:T(8,128)(2,1)S(1)}, u32[]{:S(2)}, u32[]{:S(2)}) %collective-permute-start.10) | collective-permute-done | bytes 65568 | tf_op jit(solution)/shard_map/ppermute | solution.py:234
  64.2 1.3 %collective-permute-start.7 = (bf16[2,512,512]{2,1,0:T(8,128)(2,1)S(1)}, bf16[2,512,512]{2,1,0:T(8,128)(2,1)S(1)}, u32[]{:S(2)}, u32[]{:S(2)}) collective-permute-start(bf16[2,512,512]{2,1,0:T(8,128)(2,1)S(1)} %get-tuple-element.12), channel_id=1, source_target_pairs={{8,0},{24,16},{40,32},{56,48},{72,64},{88,80},{104,96},{120,112},{... | collective-permute-start | bytes 3145736 | tf_op jit(solution)/shard_map/ppermute | solution.py:237
  65.5 1.5 %collective-permute-start.15 = (bf16[2,512,512]{2,1,0:T(8,128)(2,1)S(1)}, bf16[2,512,512]{2,1,0:T(8,128)(2,1)S(1)}, u32[]{:S(2)}, u32[]{:S(2)}) collective-permute-start(bf16[2,512,512]{2,1,0:T(8,128)(2,1)S(1)} %collective-permute-done.14.refs_0_), channel_id=1, source_target_pairs={{0,8},{8,0},{16,24},{24,16},{32,40},{40,32},{48,56},{56,48},{64,72... | collective-permute-start | bytes 3145736 | tf_op jit(solution)/shard_map/ppermute | solution.py:237
  67.0 9.2 %collective-permute-done.11.refs_1_ = bf16[4,512,128]{2,1,0:T(8,128)(2,1)S(1)} collective-permute-done((bf16[4,512,128]{2,1,0:T(8,128)(2,1)S(1)}, bf16[4,512,128]{2,1,0:T(8,128)(2,1)S(1)}, u32[]{:S(2)}, u32[]{:S(2)}) %collective-permute-start.11) | collective-permute-done | bytes 524320 | tf_op jit(solution)/shard_map/ppermute | solution.py:241
  76.2 3.4 %collective-permute-done.12.refs_2_ = bf16[4,512,128]{2,1,0:T(8,128)(2,1)S(1)} collective-permute-done((bf16[4,512,128]{2,1,0:T(8,128)(2,1)S(1)}, bf16[4,512,128]{2,1,0:T(8,128)(2,1)S(1)}, u32[]{:S(2)}, u32[]{:S(2)}) %collective-permute-start.12) | collective-permute-done | bytes 524320 | tf_op jit(solution)/shard_map/ppermute | solution.py:241
  79.5 1.2 %shard_map.49.refs_2_ = f32[2,512,512]{2,1,0:T(8,128)S(1)} custom-call(bf16[4,512,128]{2,1,0:T(8,128)(2,1)S(1)} %collective-permute-done.8.refs_0_, bf16[4,512,128]{2,1,0:T(8,128)(2,1)S(1)} %collective-permute-done.11.refs_1_, bf16[4,512,128]{2,1,0:T(8,128)(2,1)S(1)} %collective-permute-done.12.refs_2_, ...), custom_call_target="tpu_custom_call" | custom-call | flops 1020000000 | bytes 3000000 | tf_op jit(solution)/shard_map/pallas_call | solution.py:176
  80.8 0.7 shard_map.50.refs_0_
  81.5 1.4 %collective-permute-start.13 = (bf16[2,512,512]{2,1,0:T(8,128)(2,1)S(1)}, bf16[2,512,512]{2,1,0:T(8,128)(2,1)S(1)}, u32[]{:S(2)}, u32[]{:S(2)}) collective-permute-start(bf16[2,512,512]{2,1,0:T(8,128)(2,1)S(1)} %shard_map.50.refs_0_), channel_id=1, source_target_pairs={{0,8},{16,24},{32,40},{48,56},{64,72},{80,88},{96,104},{112,120},{... | collective-permute-start | bytes 3145736 | tf_op jit(solution)/shard_map/ppermute | solution.py:237
  82.8 3.1 %shard_map.51 = (bf16[2,512,512]{2,1,0:T(8,128)(2,1)S(1)}, bf16[2,128,128]{2,1,0:T(8,128)(2,1)}) custom-call(s32[1,2]{1,0:T(1,128)} %pairs_ref.3, s32[1]{0:T(128)} %bitcast.1.mom_ref, bf16[4,512,256]{2,1,0:T(8,128)(2,1)S(1)} %get-tuple-element.10.phi, bf16[4,512,256]{2,1,0:T(8,128)(2,1)S(1)} %get-tuple-element.11.rho, bf16[1,1,2,128,128]{4,3,2,1,0:T(8,128)(2,1)} %own_hbm.3, ...), custom_call_target="tpu_custom_call" | custom-call | flops 1340000000 | bytes 3000000 | tf_op jit(solution)/shard_map/pallas_call | solution.py:149
  85.9 2.0 %shard_map.52.refs_2_ = bf16[1,4,1,2,512,512]{5,4,3,2,1,0:T(8,128)(2,1)} custom-call(s32[1]{0:T(128)} %bitcast.time_ref, bf16[2,512,512]{2,1,0:T(8,128)(2,1)S(1)} %collective-permute-done.14.refs_0_, bf16[2,512,512]{2,1,0:T(8,128)(2,1)S(1)} %get-tuple-element.14.refs_1_.refs_2_), custom_call_target="tpu_custom_call" | custom-call | flops 1080000000 | bytes 3000000 | tf_op jit(solution)/shard_map/pallas_call | solution.py:215
  87.9 2.0 %shard_map.53.refs_2_ = bf16[1,4,1,2,512,512]{5,4,3,2,1,0:T(8,128)(2,1)} custom-call(s32[1]{0:T(128)} %bitcast.time_ref, bf16[2,512,512]{2,1,0:T(8,128)(2,1)S(1)} %shard_map.50.refs_0_, bf16[2,512,512]{2,1,0:T(8,128)(2,1)S(1)} %get-tuple-element.14.refs_1_.refs_2_, bf16[1,4,1,2,512,512]{5,4,3,2,1,0:T(8,128)(2,1)} %shard_map.52.refs_2_), custom_call_target="tpu_custom_call", output_to_operand_aliasing={{}: (3, {})} | custom-call | flops 1080000000 | bytes 3000000 | tf_op jit(solution)/shard_map/pallas_call | solution.py:215
  90.0 2.0 %shard_map.54.refs_3_ = bf16[1,4,1,2,512,512]{5,4,3,2,1,0:T(8,128)(2,1)} custom-call(s32[1]{0:T(128)} %bitcast.time_ref, bf16[2,512,512]{2,1,0:T(8,128)(2,1)S(1)} %collective-permute-done.15.refs_0_, bf16[2,512,512]{2,1,0:T(8,128)(2,1)S(1)} %get-tuple-element.14.refs_1_.refs_2_, ...), custom_call_target="tpu_custom_call", output_to_operand_aliasing={{}: (3, {})} | custom-call | flops 1080000000 | bytes 3000000 | tf_op jit(solution)/shard_map/pallas_call | solution.py:215
  92.0 2.0 %shard_map.55 = bf16[1,4,1,2,512,512]{5,4,3,2,1,0:T(8,128)(2,1)} custom-call(s32[1]{0:T(128)} %bitcast.time_ref, bf16[2,512,512]{2,1,0:T(8,128)(2,1)S(1)} %collective-permute-done.7.refs_0_, bf16[2,512,512]{2,1,0:T(8,128)(2,1)S(1)} %collective-permute-done.13.refs_1_, ...), custom_call_target="tpu_custom_call", output_to_operand_aliasing={{}: (4, {})} | custom-call | flops 1080000000 | bytes 3000000 | tf_op jit(solution)/shard_map/pallas_call | solution.py:215
  (10 shorter events, 0.0 us)
Async XLA Ops:
  0.0 6.0 %collective-permute-start.3 = (bf16[2,128,128]{2,1,0:T(8,128)(2,1)}, bf16[2,128,128]{2,1,0:T(8,128)(2,1)S(1)}, u32[]{:S(2)}, u32[]{:S(2)}) collective-permute-start(bf16[2,128,128]{2,1,0:T(8,128)(2,1)} %bitcast.3), channel_id=1, source_target_pairs={{0,1},{1,0},{2,3},{3,2},{4,5},{5,4},{6,7},{7,6},{8,9},{9,8},{10,11... | collective-permute-start | bytes 196616 | tf_op jit(solution)/shard_map/ppermute | solution.py:244
  0.3 8.5 %collective-permute-start = (bf16[2,128,128]{2,1,0:T(8,128)(2,1)}, bf16[2,128,128]{2,1,0:T(8,128)(2,1)S(1)}, u32[]{:S(2)}, u32[]{:S(2)}) collective-permute-start(bf16[2,128,128]{2,1,0:T(8,128)(2,1)} %bitcast.4), channel_id=1, source_target_pairs={{0,2},{1,3},{2,4},{3,5},{4,6},{5,7},{6,0},{7,1},{8,10},{9,11},{10,... | collective-permute-start | bytes 196616 | tf_op jit(solution)/shard_map/ppermute | solution.py:241
  2.5 9.3 %collective-permute-start.1 = (bf16[2,128,128]{2,1,0:T(8,128)(2,1)}, bf16[2,128,128]{2,1,0:T(8,128)(2,1)S(1)}, u32[]{:S(2)}, u32[]{:S(2)}) collective-permute-start(bf16[2,128,128]{2,1,0:T(8,128)(2,1)} %bitcast.5), channel_id=1, source_target_pairs={{0,4},{1,5},{2,6},{3,7},{4,0},{5,1},{6,2},{7,3},{8,12},{9,13},{10,... | collective-permute-start | bytes 196616 | tf_op jit(solution)/shard_map/ppermute | solution.py:241
  3.2 8.6 %collective-permute-start.2 = (bf16[2,128,128]{2,1,0:T(8,128)(2,1)}, bf16[2,128,128]{2,1,0:T(8,128)(2,1)S(1)}, u32[]{:S(2)}, u32[]{:S(2)}) collective-permute-start(bf16[2,128,128]{2,1,0:T(8,128)(2,1)} %bitcast.6), channel_id=1, source_target_pairs={{0,6},{1,7},{2,0},{3,1},{4,2},{5,3},{6,4},{7,5},{8,14},{9,15},{10,... | collective-permute-start | bytes 196616 | tf_op jit(solution)/shard_map/ppermute | solution.py:241
  6.0 5.9 %collective-permute-start.4 = (bf16[2,128,128]{2,1,0:T(8,128)(2,1)S(1)}, bf16[2,128,128]{2,1,0:T(8,128)(2,1)S(1)}, u32[]{:S(2)}, u32[]{:S(2)}) collective-permute-start(bf16[2,128,128]{2,1,0:T(8,128)(2,1)S(1)} %collective-permute-done.3.refs_3_), channel_id=1, source_target_pairs={{0,2},{1,3},{2,4},{3,5},{4,6},{5,7},{6,0},{7,1},{8,10},{9,11},{10,... | collective-permute-start | bytes 196616 | tf_op jit(solution)/shard_map/ppermute | solution.py:241
  6.5 5.8 %collective-permute-start.5 = (bf16[2,128,128]{2,1,0:T(8,128)(2,1)S(1)}, bf16[2,128,128]{2,1,0:T(8,128)(2,1)S(1)}, u32[]{:S(2)}, u32[]{:S(2)}) collective-permute-start(bf16[2,128,128]{2,1,0:T(8,128)(2,1)S(1)} %collective-permute-done.3.refs_3_), channel_id=1, source_target_pairs={{0,4},{1,5},{2,6},{3,7},{4,0},{5,1},{6,2},{7,3},{8,12},{9,13},{10,... | collective-permute-start | bytes 196616 | tf_op jit(solution)/shard_map/ppermute | solution.py:241
  8.9 5.5 %collective-permute-start.6 = (bf16[2,128,128]{2,1,0:T(8,128)(2,1)S(1)}, bf16[2,128,128]{2,1,0:T(8,128)(2,1)S(1)}, u32[]{:S(2)}, u32[]{:S(2)}) collective-permute-start(bf16[2,128,128]{2,1,0:T(8,128)(2,1)S(1)} %collective-permute-done.3.refs_3_), channel_id=1, source_target_pairs={{0,6},{1,7},{2,0},{3,1},{4,2},{5,3},{6,4},{7,5},{8,14},{9,15},{10,... | collective-permute-start | bytes 196616 | tf_op jit(solution)/shard_map/ppermute | solution.py:241
  17.4 48.0 %collective-permute-start.14 = (bf16[2,512,512]{2,1,0:T(8,128)(2,1)S(1)}, bf16[2,512,512]{2,1,0:T(8,128)(2,1)S(1)}, u32[]{:S(2)}, u32[]{:S(2)}) collective-permute-start(bf16[2,512,512]{2,1,0:T(8,128)(2,1)S(1)} %get-tuple-element.12), channel_id=1, source_target_pairs={{0,240},{8,248},{16,0},{24,8},{32,16},{40,24},{48,32},{56,40},{64,... | collective-permute-start | bytes 3145736 | tf_op jit(solution)/shard_map/ppermute | solution.py:234
  24.1 30.8 %collective-permute-start.8 = (bf16[4,512,128]{2,1,0:T(8,128)(2,1)S(1)}, bf16[4,512,128]{2,1,0:T(8,128)(2,1)S(1)}, u32[]{:S(2)}, u32[]{:S(2)}) collective-permute-start(bf16[4,512,128]{2,1,0:T(8,128)(2,1)S(1)} %shard_map.48), channel_id=1, source_target_pairs={{0,224},{8,232},{16,240},{24,248},{32,0},{40,8},{48,16},{56,24},{6... | collective-permute-start | bytes 1572872 | tf_op jit(solution)/shard_map/ppermute | solution.py:234
  54.9 21.3 %collective-permute-start.11 = (bf16[4,512,128]{2,1,0:T(8,128)(2,1)S(1)}, bf16[4,512,128]{2,1,0:T(8,128)(2,1)S(1)}, u32[]{:S(2)}, u32[]{:S(2)}) collective-permute-start(bf16[4,512,128]{2,1,0:T(8,128)(2,1)S(1)} %collective-permute-done.8.refs_0_), channel_id=1, source_target_pairs={{0,2},{1,3},{2,4},{3,5},{4,6},{5,7},{6,0},{7,1},{8,10},{9,11},{10,... | collective-permute-start | bytes 1572872 | tf_op jit(solution)/shard_map/ppermute | solution.py:241
  56.5 23.0 %collective-permute-start.12 = (bf16[4,512,128]{2,1,0:T(8,128)(2,1)S(1)}, bf16[4,512,128]{2,1,0:T(8,128)(2,1)S(1)}, u32[]{:S(2)}, u32[]{:S(2)}) collective-permute-start(bf16[4,512,128]{2,1,0:T(8,128)(2,1)S(1)} %collective-permute-done.8.refs_0_), channel_id=1, source_target_pairs={{0,6},{1,7},{2,0},{3,1},{4,2},{5,3},{6,4},{7,5},{8,14},{9,15},{10,... | collective-permute-start | bytes 1572872 | tf_op jit(solution)/shard_map/ppermute | solution.py:241
  56.9 23.8 %collective-permute-start.9 = (bf16[4,512,128]{2,1,0:T(8,128)(2,1)S(1)}, bf16[4,512,128]{2,1,0:T(8,128)(2,1)S(1)}, u32[]{:S(2)}, u32[]{:S(2)}) collective-permute-start(bf16[4,512,128]{2,1,0:T(8,128)(2,1)S(1)} %collective-permute-done.8.refs_0_), channel_id=1, source_target_pairs={{0,4},{1,5},{2,6},{3,7},{4,0},{5,1},{6,2},{7,3},{8,12},{9,13},{10,... | collective-permute-start | bytes 1572872 | tf_op jit(solution)/shard_map/ppermute | solution.py:241
  58.6 5.6 %collective-permute-start.10 = (bf16[2,128,128]{2,1,0:T(8,128)(2,1)S(1)}, bf16[2,128,128]{2,1,0:T(8,128)(2,1)S(1)}, u32[]{:S(2)}, u32[]{:S(2)}) collective-permute-start(bf16[2,128,128]{2,1,0:T(8,128)(2,1)S(1)} %get-tuple-element.13), channel_id=1, source_target_pairs={{0,224},{8,232},{16,240},{24,248},{32,0},{40,8},{48,16},{56,24},{6... | collective-permute-start | bytes 196616 | tf_op jit(solution)/shard_map/ppermute | solution.py:234
  64.2 27.8 %collective-permute-start.7 = (bf16[2,512,512]{2,1,0:T(8,128)(2,1)S(1)}, bf16[2,512,512]{2,1,0:T(8,128)(2,1)S(1)}, u32[]{:S(2)}, u32[]{:S(2)}) collective-permute-start(bf16[2,512,512]{2,1,0:T(8,128)(2,1)S(1)} %get-tuple-element.12), channel_id=1, source_target_pairs={{8,0},{24,16},{40,32},{56,48},{72,64},{88,80},{104,96},{120,112},{... | collective-permute-start | bytes 3145736 | tf_op jit(solution)/shard_map/ppermute | solution.py:237
  65.5 24.5 %collective-permute-start.15 = (bf16[2,512,512]{2,1,0:T(8,128)(2,1)S(1)}, bf16[2,512,512]{2,1,0:T(8,128)(2,1)S(1)}, u32[]{:S(2)}, u32[]{:S(2)}) collective-permute-start(bf16[2,512,512]{2,1,0:T(8,128)(2,1)S(1)} %collective-permute-done.14.refs_0_), channel_id=1, source_target_pairs={{0,8},{8,0},{16,24},{24,16},{32,40},{40,32},{48,56},{56,48},{64,72... | collective-permute-start | bytes 3145736 | tf_op jit(solution)/shard_map/ppermute | solution.py:237
  81.5 10.6 %collective-permute-start.13 = (bf16[2,512,512]{2,1,0:T(8,128)(2,1)S(1)}, bf16[2,512,512]{2,1,0:T(8,128)(2,1)S(1)}, u32[]{:S(2)}, u32[]{:S(2)}) collective-permute-start(bf16[2,512,512]{2,1,0:T(8,128)(2,1)S(1)} %shard_map.50.refs_0_), channel_id=1, source_target_pairs={{0,8},{16,24},{32,40},{48,56},{64,72},{80,88},{96,104},{112,120},{... | collective-permute-start | bytes 3145736 | tf_op jit(solution)/shard_map/ppermute | solution.py:237

commit v2 on v1

v2 whole, which is shorter than its diff:
```python
import functools

import jax
import jax.numpy as jnp
from jax import lax
from jax.experimental import pallas as pl
from jax.experimental.pallas import tpu as pltpu
from jax.sharding import PartitionSpec as P


NSEP = 4
VMEM_LIMIT = 24 * 1024 * 1024
F32 = jnp.float32
BF16 = jnp.bfloat16
VMEM, SMEM, HBM = pltpu.VMEM, pltpu.SMEM, pltpu.HBM
DMA = pltpu.SemaphoreType.DMA


def transpose_product(left_mat, right_mat):
    return lax.dot_general(
        left_mat, right_mat, (((1,), (1,)), ((), ())), preferred_element_type=F32
    )


def in_space(space, count=1):
    return [pl.BlockSpec(memory_space=space)] * count


def fixed(array, space):
    return pltpu.with_memory_space_constraint(array, space)


def kernel_call(body, flops, in_specs, out_shape, scratch=(), **options):
    many = isinstance(out_shape, list)
    spaces = [in_space(shape.memory_space)[0] for shape in (out_shape if many else [out_shape])]
    return pl.pallas_call(
        body,
        in_specs=in_specs,
        out_specs=spaces if many else spaces[0],
        out_shape=out_shape,
        scratch_shapes=scratch,
        compiler_params=pltpu.CompilerParams(vmem_limit_bytes=VMEM_LIMIT),
        cost_estimate=pl.CostEstimate(flops=flops, bytes_accessed=3_000_000, transcendentals=0),
        **options,
    )


def outgoing_kernel(phi_hbm, rho_hbm, phi_out, rho_out, sems):
    nev = phi_out.shape[2]
    cols = pl.ds(pl.multiple_of(lax.axis_index("mom") // 2 * nev, nev), nev)
    copies = []
    for source, held in ((phi_hbm, phi_out), (rho_hbm, rho_out)):
        for part in range(2):
            copies.append(
                pltpu.make_async_copy(source.at[0, part, :, cols], held.at[part], sems.at[len(copies)])
            )
            copies[-1].start()
    for copy in copies:
        copy.wait()


def outgoing(sink, noise, nev):
    rows = sink.shape[2]
    return kernel_call(
        outgoing_kernel, 1_000_000, in_space(HBM, 2), [VMEM((2, rows, nev), BF16)] * 2, [DMA((4,))]
    )(fixed(sink, HBM), fixed(noise, HBM))


def by_spin(source, held, sems):
    spins, nev = held.shape[0], held.shape[2] // 2
    return [
        pltpu.make_async_copy(
            source.at[0, part, :, pl.ds(spin * nev, nev)],
            held.at[spin, :, pl.ds(part * nev, nev)],
            sems.at[2 * spin + part],
        )
        for spin in range(spins)
        for part in range(2)
    ]


def stage_kernel(phi_hbm, rho_hbm, elem_hbm, phi, rho, elem, sems):
    count = sems.shape[0] // 2
    copies = by_spin(phi_hbm, phi, sems) + by_spin(rho_hbm, rho, sems.at[pl.ds(count, count)])
    copies.append(pltpu.make_async_copy(elem_hbm.at[0, 0], elem, sems.at[2 * count]))
    for copy in copies:
        copy.start()
    for copy in copies:
        copy.wait()


def stage(sink, noise, elementals):
    rows, width = sink.shape[2:]
    nev = elementals.shape[3]
    spins = width // nev
    return kernel_call(
        stage_kernel,
        1_000_000,
        in_space(HBM, 3),
        [VMEM((spins, rows, 2 * nev), BF16)] * 2 + [VMEM((2, nev, nev), BF16)],
        [DMA((4 * spins + 1,))],
    )(fixed(sink, HBM), fixed(noise, HBM), fixed(elementals, HBM))


def paired_kernel(own_ref, across_ref, out_ref):
    out_ref[0] = own_ref[...]
    out_ref[1] = across_ref[...]


def paired(own, across):
    return kernel_call(
        paired_kernel, 1_000_000, in_space(VMEM, 2), VMEM((2, *own.shape), BF16)
    )(own, across)


def fill_weights(elem, weights):
    nev = elem.shape[1]
    re, im = elem[0], elem[1]
    weights[:nev, :nev], weights[:nev, nev:] = re, -im
    weights[nev:, :nev], weights[nev:, nev:] = im, re


def apply_elemental(phi, weights, right, at):
    nev = phi.shape[1] // 2
    applied = transpose_product(weights, phi).astype(BF16)
    right[0, at : at + 2 * nev] = applied
    right[1, at : at + nev] = applied[nev:]
    right[1, at + nev : at + 2 * nev] = -applied[:nev]


def plain_product(left, right):
    return jnp.dot(left, right, preferred_element_type=F32)


def choose(wanted, held_elems, chosen):
    columns, mom = len(held_elems), lax.axis_index("mom")
    distance = lax.rem(mom // 2 - wanted // 2 + columns, columns)
    for index, elem in enumerate(held_elems):
        for across in range(2):
            @pl.when((distance == index) & (lax.rem(wanted + mom, 2) == across))
            def _():
                chosen[...] = elem[across]


def apply_all(phi, chosen, weights, right):
    fill_weights(chosen, weights)
    for spin in range(phi.shape[0]):
        apply_elemental(phi[spin], weights[...], right, spin * phi.shape[2])


def noise_rows(rho, first, rows):
    lines = slice(first, first + rows)
    return jnp.concatenate([rho[spin, lines] for spin in range(rho.shape[0])], axis=1)


def upper_sink_kernel(columns, pairs_ref, phi, rho, *refs):
    held_elems = refs[:columns]
    upper, right, chosen, weights = refs[columns:]
    choose(pairs_ref[0, 0], held_elems, chosen)
    apply_all(phi, chosen, weights, right)
    left = noise_rows(rho, 0, upper.shape[1])
    for part in range(2):
        upper[part] = plain_product(left, right[part]).astype(BF16)


def upper_sink(pairs, phi, rho, elementals, upper_rows):
    spins, rows, nev = phi.shape[0], phi.shape[1], phi.shape[2] // 2
    return kernel_call(
        functools.partial(upper_sink_kernel, len(elementals)),
        800_000_000,
        in_space(SMEM) + in_space(VMEM, 2 + len(elementals)),
        [
            VMEM((2, upper_rows, rows), BF16),
            VMEM((2, spins * 2 * nev, rows), BF16),
            VMEM((2, nev, nev), BF16),
        ],
        [VMEM((2 * nev, 2 * nev), BF16)],
    )(fixed(pairs, HBM), phi, rho, *elementals)


def lower_sink_kernel(rho, right, upper, lower, full):
    first, rows = upper.shape[1], lower.shape[1]
    left = noise_rows(rho, first, rows)
    for part in range(2):
        term = plain_product(left, right[part]).astype(BF16)
        lower[part] = term
        full[part, first:] = term
        full[part, :first] = upper[part]


def lower_sink(rho, right, upper):
    rows = rho.shape[1]
    return kernel_call(
        lower_sink_kernel,
        540_000_000,
        in_space(VMEM, 3),
        [VMEM((2, rows - upper.shape[1], rows), BF16), VMEM((2, rows, rows), BF16)],
    )(rho, right, upper)


def source_kernel(columns, pairs_ref, phi, rho, *refs):
    held_elems = refs[:columns]
    out_ref, chosen, weights, right = refs[columns:]
    choose(pairs_ref[0, 1], held_elems, chosen)
    apply_all(phi, chosen, weights, right)
    left = noise_rows(rho, 0, out_ref.shape[1])
    for part in range(2):
        out_ref[part] = plain_product(left, right[part]).astype(BF16)


def source(pairs, phi, rho, elementals):
    spins, rows, nev = phi.shape[0], phi.shape[1], phi.shape[2] // 2
    return kernel_call(
        functools.partial(source_kernel, len(elementals)),
        1_340_000_000,
        in_space(SMEM) + in_space(VMEM, 2 + len(elementals)),
        VMEM((2, rows, rows), BF16),
        [
            VMEM((2, nev, nev), BF16),
            VMEM((2 * nev, 2 * nev), BF16),
            VMEM((2, spins * 2 * nev, rows), BF16),
        ],
    )(fixed(pairs, HBM), phi, rho, *elementals)


def applied_kernel(*refs):
    *pieces, elem_ref, right, weights = refs
    nev = elem_ref.shape[1]
    fill_weights(elem_ref, weights)
    for index, piece in enumerate(pieces):
        phi = jnp.concatenate([piece[0], piece[1]], axis=1)
        apply_elemental(phi, weights[...], right, index * 2 * nev)


def applied(pieces, elemental):
    rows, nev = pieces[0].shape[1:]
    operands = [*pieces, elemental]
    return kernel_call(
        applied_kernel,
        270_000_000,
        in_space(VMEM, len(operands)),
        VMEM((2, 2 * nev * len(pieces), rows), BF16),
        [VMEM((2 * nev, 2 * nev), BF16)],
    )(*operands)


def noise_kernel(*refs):
    *pieces, right, out_ref = refs
    left = jnp.concatenate([piece[part] for piece in pieces for part in range(2)], axis=1)
    for part in range(2):
        out_ref[part] = plain_product(left, right[part]).astype(BF16)


def noise_product(pieces, right):
    rows = pieces[0].shape[1]
    return kernel_call(
        noise_kernel, 1_080_000_000, in_space(VMEM, len(pieces) + 1), VMEM((2, rows, rows), BF16)
    )(*pieces, right)


def product_kernel(jobs, *refs):
    right = refs[sum(choices for _, _, choices in jobs)]
    out_hbm, held, sems = refs[-3:]
    core = lax.rem(lax.axis_index("tm"), 2)
    copies = []
    taken = 0
    for job, (place, first, choices) in enumerate(jobs):
        lefts = refs[taken : taken + choices]
        taken += choices
        rows = lefts[0].shape[1]
        size = rows // 2 if job + 1 == len(jobs) else rows
        for start in range(0, rows, size):
            lines = pl.ds(start, size)
            left = [ref[:, lines] for ref in lefts]
            left = left[0] if choices == 1 else jnp.where(core == 0, *left)
            for part in range(2):
                if part == 0:
                    term = plain_product(left[0], right[0]) - plain_product(left[1], right[1])
                else:
                    term = plain_product(left[0], right[1]) + plain_product(left[1], right[0])
                held[job, part, lines] = term.astype(BF16)
                copies.append(
                    pltpu.make_async_copy(
                        held.at[job, part, lines],
                        out_hbm.at[0, place(core), 0, part, pl.ds(first + start, size)],
                        sems.at[len(copies)],
                    )
                )
                copies[-1].start()
    for copy in copies:
        copy.wait()


def product(jobs, right, blocks):
    rows = right.shape[1]
    lefts = [left for _, _, lefts in jobs for left in lefts]
    operands = [*lefts, right] + ([] if blocks is None else [blocks])
    return kernel_call(
        functools.partial(
            product_kernel, tuple((place, first, len(lefts)) for place, first, lefts in jobs)
        ),
        sum(2_100_000 * jobs[i][2][0].shape[1] for i in range(len(jobs))),
        in_space(VMEM, len(lefts) + 1) + ([] if blocks is None else in_space(pl.ANY)),
        HBM((1, NSEP, 1, 2, rows, rows), BF16),
        [VMEM((len(jobs), 2, rows, rows), BF16), DMA((4 * len(jobs),))],
        input_output_aliases={} if blocks is None else {len(operands) - 1: 0},
    )(*operands)


def local(sink, noise, elementals, pairs):
    times, moms = lax.axis_size("tm"), lax.axis_size("mom")
    nev = elementals.shape[3]
    columns = moms // 2

    def earlier(block, distance):
        return lax.ppermute(block, "tm", [(t, (t - distance) % times) for t in range(times)])

    def partner(block):
        return lax.ppermute(block, "tm", [(t, t ^ 1) for t in range(times)])

    def along_x(block, distance):
        route = [(m, (m // 2 + distance) % columns * 2 + m % 2) for m in range(moms)]
        return lax.ppermute(block, "mom", route)

    own = elementals[0, 0]
    across = lax.ppermute(own, "mom", [(m, m ^ 1) for m in range(moms)])
    phi, rho = outgoing(sink, noise, nev)
    phi = earlier(phi, 4)
    rho = earlier(rho, 4)
    own_phi, own_rho, own = stage(sink, noise, elementals)
    elems = [paired(own, across)]
    for distance in (1, 2, 3):
        elems.append(along_x(elems[0], distance))
    phis, rhos = [phi], [rho]
    for distance in (1, 3, 2):
        phis.append(along_x(phi, distance))
    for distance in (1, 3, 2):
        rhos.append(along_x(rho, distance))

    upper_rows = own_phi.shape[1] * 5 // 8
    upper, sink_right, sink_elemental = upper_sink(pairs, own_phi, own_rho, elems, upper_rows)
    later_elemental = earlier(sink_elemental, 4)
    two_a = earlier(upper, 2)
    lower, sink_meson = lower_sink(own_rho, sink_right, upper)
    two_b = earlier(lower, 2)
    beside = partner(sink_meson)
    source_meson = source(pairs, own_phi, own_rho, elems)

    beside_a = partner(two_a)
    right = applied(phis, later_elemental)
    four_later = noise_product(rhos, right)
    beside_four = partner(four_later)
    beside_b = partner(two_b)

    two, one_or_three, four, three_or_one = (
        lambda c: 1, lambda c: 2 * c, lambda c: 3, lambda c: 2 - 2 * c,
    )
    blocks = product([(two, 0, [two_a])], source_meson, None)
    jobs = [(four, 0, [four_later]), (three_or_one, 0, [beside_a])]
    blocks = product(jobs, source_meson, blocks)
    jobs = [(one_or_three, 0, [beside, beside_four]), (two, upper_rows, [two_b])]
    blocks = product(jobs, source_meson, blocks)
    return product([(three_or_one, upper_rows, [beside_b])], source_meson, blocks)


def solution(mesh):
    return jax.shard_map(
        local,
        mesh=mesh,
        in_specs=(
            P("tm", None, None, None),
            P("tm", None, None, None),
            P("mom", "tm", None, None, None),
            P("mom", None),
        ),
        out_specs=P("tm", None, "mom", None, None, None),
        check_vma=False,
    )
```

time: 94.5 us -> 73.8 us (0.78)
  the two profiles are of different devices: /device:TPU:22 before, /device:TPU:1 now
where the time goes in v2:
time: 73.8 us; the launch traced here: 73.7 us
  starting transfers between devices  42.6 us (58%)
  Pallas kernels  17.7 us (24%)
  waiting for transfers between devices  13.1 us (18%)
    ppermute x9, starting transfers between devices, along_x(): return lax.ppermute(block, 'mom', route)  16 us
    ppermute x4, starting transfers between devices, partner(): return lax.ppermute(block, 'tm', [(t, t ^ 1) for t in range(times)])  12.8 us
    ppermute x5, starting transfers between devices, earlier(): lax.ppermute(block, 'tm', [(t, (t - distance) % times) for t in range(tim...  10.9 us
    ppermute x5, waiting for transfers between devices, earlier(): lax.ppermute(block, 'tm', [(t, (t - distance) % times) for t in range(tim...  10 us
    pallas_call x4, Pallas kernels, product(): kernel_call(functools.partial(product_kernel, tuple(((place, first, len(l...  8.31 us
    ppermute x9, waiting for transfers between devices, along_x(): return lax.ppermute(block, 'mom', route)  2.92 us
    ppermute x1, starting transfers between devices, local(): across = lax.ppermute(own, 'mom', [(m, m ^ 1) for m in range(moms)])  2.91 us
    pallas_call x1, Pallas kernels, source(): kernel_call(functools.partial(source_kernel, len(elementals)), 1340000000...  2.27 us
  transfers between devices with their start and end apart: 19, of which 6 were waited for; matrix products, arithmetic and copies ran while one was open for 0% of the time, Pallas kernels for 20%

profile of v2, /device:TPU:1, one launch (start us, length us, event | category | flops | bytes accessed | tf_op | source)
XLA Modules:
  0.0 73.7 jit_solution(1256548407811728521)
XLA Ops:
  0.0 1.1 %shard_map.51 = (bf16[2,512,128]{2,1,0:T(8,128)(2,1)S(1)}, bf16[2,512,128]{2,1,0:T(8,128)(2,1)S(1)}) custom-call(bf16[1,2,512,512]{3,2,1,0:T(8,128)(2,1)} %phi_hbm.3, bf16[1,2,512,512]{3,2,1,0:T(8,128)(2,1)} %rho_hbm.3), custom_call_target="tpu_custom_call" | custom-call | flops 1000000 | bytes 3000000 | tf_op jit(solution)/shard_map/pallas_call | solution.py:64
  1.1 6.5 %collective-permute-start.11 = (bf16[2,512,128]{2,1,0:T(8,128)(2,1)S(1)}, bf16[2,512,128]{2,1,0:T(8,128)(2,1)S(1)}, u32[]{:S(2)}, u32[]{:S(2)}) collective-permute-start(bf16[2,512,128]{2,1,0:T(8,128)(2,1)S(1)} %get-tuple-element.23), channel_id=1, source_target_pairs={{0,224},{8,232},{16,240},{24,248},{32,0},{40,8},{48,16},{56,24},{6... | collective-permute-start | bytes 786440 | tf_op jit(solution)/shard_map/ppermute | solution.py:316
  7.6 2.9 %collective-permute-start = (bf16[2,128,128]{2,1,0:T(8,128)(2,1)}, bf16[2,128,128]{2,1,0:T(8,128)(2,1)S(1)}, u32[]{:S(2)}, u32[]{:S(2)}) collective-permute-start(bf16[2,128,128]{2,1,0:T(8,128)(2,1)} %bitcast.1), channel_id=1, source_target_pairs={{0,1},{1,0},{2,3},{3,2},{4,5},{5,4},{6,7},{7,6},{8,9},{9,8},{10,11... | collective-permute-start | bytes 196616 | tf_op jit(solution)/shard_map/ppermute | solution.py:326
  10.5 1.8 %shard_map.46 = (bf16[4,512,256]{2,1,0:T(8,128)(2,1)S(1)}, bf16[4,512,256]{2,1,0:T(8,128)(2,1)S(1)}, bf16[2,128,128]{2,1,0:T(8,128)(2,1)S(1)}) custom-call(bf16[1,2,512,512]{3,2,1,0:T(8,128)(2,1)} %phi_hbm.3, bf16[1,2,512,512]{3,2,1,0:T(8,128)(2,1)} %rho_hbm.3, bf16[1,1,2,128,128]{4,3,2,1,0:T(8,128)(2,1)} %elem_hbm.1), custom_call_target="tpu_custom_call" | custom-call | flops 1000000 | bytes 3000000 | tf_op jit(solution)/shard_map/pallas_call | solution.py:96
  12.5 2.6 %collective-permute-start.3 = (bf16[2,2,128,128]{3,2,1,0:T(8,128)(2,1)S(1)}, bf16[2,2,128,128]{3,2,1,0:T(8,128)(2,1)S(1)}, u32[]{:S(2)}, u32[]{:S(2)}) collective-permute-start(bf16[2,2,128,128]{3,2,1,0:T(8,128)(2,1)S(1)} %shard_map.47.refs_0_), channel_id=1, source_target_pairs={{0,6},{1,7},{2,0},{3,1},{4,2},{5,3},{6,4},{7,5},{8,14},{9,15},{10,... | collective-permute-start | bytes 393224 | tf_op jit(solution)/shard_map/ppermute | solution.py:323
  15.0 0.7 collective-permute-start.7
  15.7 0.5 collective-permute-start.2
  16.3 0.6 collective-permute-start.1
  16.9 1.8 %collective-permute-start.14 = (bf16[2,512,128]{2,1,0:T(8,128)(2,1)S(1)}, bf16[2,512,128]{2,1,0:T(8,128)(2,1)S(1)}, u32[]{:S(2)}, u32[]{:S(2)}) collective-permute-start(bf16[2,512,128]{2,1,0:T(8,128)(2,1)S(1)} %collective-permute-done.11.refs_0_), channel_id=1, source_target_pairs={{0,4},{1,5},{2,6},{3,7},{4,0},{5,1},{6,2},{7,3},{8,12},{9,13},{10,... | collective-permute-start | bytes 786440 | tf_op jit(solution)/shard_map/ppermute | solution.py:323
  18.7 2.1 %collective-permute-start.13 = (bf16[2,512,128]{2,1,0:T(8,128)(2,1)S(1)}, bf16[2,512,128]{2,1,0:T(8,128)(2,1)S(1)}, u32[]{:S(2)}, u32[]{:S(2)}) collective-permute-start(bf16[2,512,128]{2,1,0:T(8,128)(2,1)S(1)} %collective-permute-done.11.refs_0_), channel_id=1, source_target_pairs={{0,6},{1,7},{2,0},{3,1},{4,2},{5,3},{6,4},{7,5},{8,14},{9,15},{10,... | collective-permute-start | bytes 786440 | tf_op jit(solution)/shard_map/ppermute | solution.py:323
  21.2 1.3 %collective-permute-done.1.refs_1_ = bf16[2,2,128,128]{3,2,1,0:T(8,128)(2,1)S(1)} collective-permute-done((bf16[2,2,128,128]{3,2,1,0:T(8,128)(2,1)S(1)}, bf16[2,2,128,128]{3,2,1,0:T(8,128)(2,1)S(1)}, u32[]{:S(2)}, u32[]{:S(2)}) %collective-permute-start.1) | collective-permute-done | bytes 131104 | tf_op jit(solution)/shard_map/ppermute | solution.py:323
  22.5 1.9 %shard_map.48 = (bf16[2,320,512]{2,1,0:T(8,128)(2,1)S(1)}, bf16[2,1024,512]{2,1,0:T(8,128)(2,1)S(1)}, bf16[2,128,128]{2,1,0:T(8,128)(2,1)S(1)}) custom-call(s32[1,2]{1,0:T(1,128)} %pairs_ref.3, bf16[4,512,256]{2,1,0:T(8,128)(2,1)S(1)} %get-tuple-element.16.phi, bf16[4,512,256]{2,1,0:T(8,128)(2,1)S(1)} %get-tuple-element.15.rho, ...), custom_call_target="tpu_custom_call" | custom-call | flops 800000000 | bytes 3000000 | tf_op jit(solution)/shard_map/pallas_call | solution.py:168
  24.4 1.1 %collective-permute-start.15 = (bf16[2,128,128]{2,1,0:T(8,128)(2,1)S(1)}, bf16[2,128,128]{2,1,0:T(8,128)(2,1)S(1)}, u32[]{:S(2)}, u32[]{:S(2)}) collective-permute-start(bf16[2,128,128]{2,1,0:T(8,128)(2,1)S(1)} %get-tuple-element.24), channel_id=1, source_target_pairs={{0,224},{8,232},{16,240},{24,248},{32,0},{40,8},{48,16},{56,24},{6... | collective-permute-start | bytes 196616 | tf_op jit(solution)/shard_map/ppermute | solution.py:316
  25.4 1.4 %collective-permute-start.17 = (bf16[2,320,512]{2,1,0:T(8,128)(2,1)S(1)}, bf16[2,320,512]{2,1,0:T(8,128)(2,1)S(1)}, u32[]{:S(2)}, u32[]{:S(2)}) collective-permute-start(bf16[2,320,512]{2,1,0:T(8,128)(2,1)S(1)} %get-tuple-element.19.upper), channel_id=1, source_target_pairs={{0,240},{8,248},{16,0},{24,8},{32,16},{40,24},{48,32},{56,40},{64,... | collective-permute-start | bytes 1966088 | tf_op jit(solution)/shard_map/ppermute | solution.py:316
  26.9 0.9 %collective-permute-done.15.refs_4_ = bf16[2,128,128]{2,1,0:T(8,128)(2,1)S(1)} collective-permute-done((bf16[2,128,128]{2,1,0:T(8,128)(2,1)S(1)}, bf16[2,128,128]{2,1,0:T(8,128)(2,1)S(1)}, u32[]{:S(2)}, u32[]{:S(2)}) %collective-permute-start.15) | collective-permute-done | bytes 65568 | tf_op jit(solution)/shard_map/ppermute | solution.py:316
  27.8 0.8 %collective-permute-start.10 = (bf16[2,512,128]{2,1,0:T(8,128)(2,1)S(1)}, bf16[2,512,128]{2,1,0:T(8,128)(2,1)S(1)}, u32[]{:S(2)}, u32[]{:S(2)}) collective-permute-start(bf16[2,512,128]{2,1,0:T(8,128)(2,1)S(1)} %collective-permute-done.7.refs_0_), channel_id=1, source_target_pairs={{0,4},{1,5},{2,6},{3,7},{4,0},{5,1},{6,2},{7,3},{8,12},{9,13},{10,... | collective-permute-start | bytes 786440 | tf_op jit(solution)/shard_map/ppermute | solution.py:323
  28.7 1.1 %collective-permute-start.9 = (bf16[2,512,128]{2,1,0:T(8,128)(2,1)S(1)}, bf16[2,512,128]{2,1,0:T(8,128)(2,1)S(1)}, u32[]{:S(2)}, u32[]{:S(2)}) collective-permute-start(bf16[2,512,128]{2,1,0:T(8,128)(2,1)S(1)} %collective-permute-done.7.refs_0_), channel_id=1, source_target_pairs={{0,6},{1,7},{2,0},{3,1},{4,2},{5,3},{6,4},{7,5},{8,14},{9,15},{10,... | collective-permute-start | bytes 786440 | tf_op jit(solution)/shard_map/ppermute | solution.py:323
  29.8 1.2 %collective-permute-done.13.refs_2_ = bf16[2,512,128]{2,1,0:T(8,128)(2,1)S(1)} collective-permute-done((bf16[2,512,128]{2,1,0:T(8,128)(2,1)S(1)}, bf16[2,512,128]{2,1,0:T(8,128)(2,1)S(1)}, u32[]{:S(2)}, u32[]{:S(2)}) %collective-permute-start.13) | collective-permute-done | bytes 262176 | tf_op jit(solution)/shard_map/ppermute | solution.py:323
  31.0 6.4 %collective-permute-start.8 = (bf16[2,512,128]{2,1,0:T(8,128)(2,1)S(1)}, bf16[2,512,128]{2,1,0:T(8,128)(2,1)S(1)}, u32[]{:S(2)}, u32[]{:S(2)}) collective-permute-start(bf16[2,512,128]{2,1,0:T(8,128)(2,1)S(1)} %collective-permute-done.7.refs_0_), channel_id=1, source_target_pairs={{0,2},{1,3},{2,4},{3,5},{4,6},{5,7},{6,0},{7,1},{8,10},{9,11},{10,... | collective-permute-start | bytes 786440 | tf_op jit(solution)/shard_map/ppermute | solution.py:323
  37.4 0.6 shard_map.49
  38.0 5.7 %collective-permute-start.6 = (bf16[2,512,512]{2,1,0:T(8,128)(2,1)S(1)}, bf16[2,512,512]{2,1,0:T(8,128)(2,1)S(1)}, u32[]{:S(2)}, u32[]{:S(2)}) collective-permute-start(bf16[2,512,512]{2,1,0:T(8,128)(2,1)S(1)} %get-tuple-element.21), channel_id=1, source_target_pairs={{0,8},{8,0},{16,24},{24,16},{32,40},{40,32},{48,56},{56,48},{64,72... | collective-permute-start | bytes 3145736 | tf_op jit(solution)/shard_map/ppermute | solution.py:319
  43.8 0.5 shard_map.52.refs_4_
  44.3 1.2 %shard_map.53.refs_0_ = bf16[2,512,512]{2,1,0:T(8,128)(2,1)S(1)} custom-call(bf16[2,512,128]{2,1,0:T(8,128)(2,1)S(1)} %collective-permute-done.7.refs_0_, bf16[2,512,128]{2,1,0:T(8,128)(2,1)S(1)} %collective-permute-done.8.refs_1_, bf16[2,512,128]{2,1,0:T(8,128)(2,1)S(1)} %collective-permute-done.9.refs_2_, ...), custom_call_target="tpu_custom_call" | custom-call | flops 1080000000 | bytes 3000000 | tf_op jit(solution)/shard_map/pallas_call | solution.py:256
  45.5 5.7 %collective-permute-start.16 = (bf16[2,512,512]{2,1,0:T(8,128)(2,1)S(1)}, bf16[2,512,512]{2,1,0:T(8,128)(2,1)S(1)}, u32[]{:S(2)}, u32[]{:S(2)}) collective-permute-start(bf16[2,512,512]{2,1,0:T(8,128)(2,1)S(1)} %shard_map.53.refs_0_), channel_id=1, source_target_pairs={{0,8},{8,0},{16,24},{24,16},{32,40},{40,32},{48,56},{56,48},{64,72... | collective-permute-start | bytes 3145736 | tf_op jit(solution)/shard_map/ppermute | solution.py:319
  51.3 1.2 %collective-permute-start.4 = (bf16[2,192,512]{2,1,0:T(8,128)(2,1)S(1)}, bf16[2,192,512]{2,1,0:T(8,128)(2,1)S(1)}, u32[]{:S(2)}, u32[]{:S(2)}) collective-permute-start(bf16[2,192,512]{2,1,0:T(8,128)(2,1)S(1)} %get-tuple-element.20), channel_id=1, source_target_pairs={{0,240},{8,248},{16,0},{24,8},{32,16},{40,24},{48,32},{56,40},{64,... | collective-permute-start | bytes 1179656 | tf_op jit(solution)/shard_map/ppermute | solution.py:316
  52.5 9.1 %collective-permute-done.4.refs_2_ = bf16[2,192,512]{2,1,0:T(8,128)(2,1)S(1)} collective-permute-done((bf16[2,192,512]{2,1,0:T(8,128)(2,1)S(1)}, bf16[2,192,512]{2,1,0:T(8,128)(2,1)S(1)}, u32[]{:S(2)}, u32[]{:S(2)}) %collective-permute-start.4) | collective-permute-done | bytes 393248 | tf_op jit(solution)/shard_map/ppermute | solution.py:316
  61.6 1.3 %collective-permute-start.5 = (bf16[2,192,512]{2,1,0:T(8,128)(2,1)S(1)}, bf16[2,192,512]{2,1,0:T(8,128)(2,1)S(1)}, u32[]{:S(2)}, u32[]{:S(2)}) collective-permute-start(bf16[2,192,512]{2,1,0:T(8,128)(2,1)S(1)} %collective-permute-done.4.refs_2_), channel_id=1, source_target_pairs={{0,8},{8,0},{16,24},{24,16},{32,40},{40,32},{48,56},{56,48},{64,72... | collective-permute-start | bytes 1179656 | tf_op jit(solution)/shard_map/ppermute | solution.py:319
  62.9 2.3 %shard_map.50.refs_1_.refs_2_.refs_3_ = bf16[2,512,512]{2,1,0:T(8,128)(2,1)S(1)} custom-call(s32[1,2]{1,0:T(1,128)} %pairs_ref.3, bf16[4,512,256]{2,1,0:T(8,128)(2,1)S(1)} %get-tuple-element.16.phi, bf16[4,512,256]{2,1,0:T(8,128)(2,1)S(1)} %get-tuple-element.15.rho, bf16[2,2,128,128]{3,2,1,0:T(8,128)(2,1)S(1)} %shard_map.47.refs_0_, ...), custom_call_target="tpu_custom_call" | custom-call | flops 1340000000 | bytes 3000000 | tf_op jit(solution)/shard_map/pallas_call | solution.py:213
  65.1 1.6 %shard_map.54.refs_3_ = bf16[1,4,1,2,512,512]{5,4,3,2,1,0:T(8,128)(2,1)} custom-call(bf16[2,320,512]{2,1,0:T(8,128)(2,1)S(1)} %collective-permute-done.17.refs_0_, bf16[2,512,512]{2,1,0:T(8,128)(2,1)S(1)} %shard_map.50.refs_1_.refs_2_.refs_3_), custom_call_target="tpu_custom_call" | custom-call | flops 672000000 | bytes 3000000 | tf_op jit(solution)/shard_map/pallas_call | solution.py:298
  66.7 2.7 %shard_map.55.refs_4_ = bf16[1,4,1,2,512,512]{5,4,3,2,1,0:T(8,128)(2,1)} custom-call(bf16[2,512,512]{2,1,0:T(8,128)(2,1)S(1)} %shard_map.53.refs_0_, bf16[2,320,512]{2,1,0:T(8,128)(2,1)S(1)} %collective-permute-done.18.refs_1_, bf16[2,512,512]{2,1,0:T(8,128)(2,1)S(1)} %shard_map.50.refs_1_.refs_2_.refs_3_, ...), custom_call_target="tpu_custom_call", output_to_operand_aliasing={{}: (3, {})} | custom-call | flops 1747200000 | bytes 3000000 | tf_op jit(solution)/shard_map/pallas_call | solution.py:298
  69.4 2.6 %shard_map.56.refs_2_ = bf16[1,4,1,2,512,512]{5,4,3,2,1,0:T(8,128)(2,1)} custom-call(bf16[2,512,512]{2,1,0:T(8,128)(2,1)S(1)} %collective-permute-done.6.refs_0_, bf16[2,512,512]{2,1,0:T(8,128)(2,1)S(1)} %collective-permute-done.16.refs_1_, bf16[2,192,512]{2,1,0:T(8,128)(2,1)S(1)} %collective-permute-done.4.refs_2_, ...), custom_call_target="tpu_custom_call", output_to_operand_aliasing={{}: (4, {})} | custom-call | flops 1478400000 | bytes 3000000 | tf_op jit(solution)/shard_map/pallas_call | solution.py:298
  72.0 1.5 %shard_map.57 = bf16[1,4,1,2,512,512]{5,4,3,2,1,0:T(8,128)(2,1)} custom-call(bf16[2,192,512]{2,1,0:T(8,128)(2,1)S(1)} %collective-permute-done.5.refs_0_, bf16[2,512,512]{2,1,0:T(8,128)(2,1)S(1)} %shard_map.50.refs_1_.refs_2_.refs_3_, bf16[1,4,1,2,512,512]{5,4,3,2,1,0:T(8,128)(2,1)} %shard_map.56.refs_2_), custom_call_target="tpu_custom_call", output_to_operand_aliasing={{}: (2, {})} | custom-call | flops 403200000 | bytes 3000000 | tf_op jit(solution)/shard_map/pallas_call | solution.py:298
  (18 shorter events, 0.6 us)
Async XLA Ops:
  1.1 15.7 %collective-permute-start.11 = (bf16[2,512,128]{2,1,0:T(8,128)(2,1)S(1)}, bf16[2,512,128]{2,1,0:T(8,128)(2,1)S(1)}, u32[]{:S(2)}, u32[]{:S(2)}) collective-permute-start(bf16[2,512,128]{2,1,0:T(8,128)(2,1)S(1)} %get-tuple-element.23), channel_id=1, source_target_pairs={{0,224},{8,232},{16,240},{24,248},{32,0},{40,8},{48,16},{56,24},{6... | collective-permute-start | bytes 786440 | tf_op jit(solution)/shard_map/ppermute | solution.py:316
  7.6 4.8 %collective-permute-start = (bf16[2,128,128]{2,1,0:T(8,128)(2,1)}, bf16[2,128,128]{2,1,0:T(8,128)(2,1)S(1)}, u32[]{:S(2)}, u32[]{:S(2)}) collective-permute-start(bf16[2,128,128]{2,1,0:T(8,128)(2,1)} %bitcast.1), channel_id=1, source_target_pairs={{0,1},{1,0},{2,3},{3,2},{4,5},{5,4},{6,7},{7,6},{8,9},{9,8},{10,11... | collective-permute-start | bytes 196616 | tf_op jit(solution)/shard_map/ppermute | solution.py:326
  12.5 6.3 %collective-permute-start.3 = (bf16[2,2,128,128]{3,2,1,0:T(8,128)(2,1)S(1)}, bf16[2,2,128,128]{3,2,1,0:T(8,128)(2,1)S(1)}, u32[]{:S(2)}, u32[]{:S(2)}) collective-permute-start(bf16[2,2,128,128]{3,2,1,0:T(8,128)(2,1)S(1)} %shard_map.47.refs_0_), channel_id=1, source_target_pairs={{0,6},{1,7},{2,0},{3,1},{4,2},{5,3},{6,4},{7,5},{8,14},{9,15},{10,... | collective-permute-start | bytes 393224 | tf_op jit(solution)/shard_map/ppermute | solution.py:323
  15.0 11.9 %collective-permute-start.7 = (bf16[2,512,128]{2,1,0:T(8,128)(2,1)S(1)}, bf16[2,512,128]{2,1,0:T(8,128)(2,1)S(1)}, u32[]{:S(2)}, u32[]{:S(2)}) collective-permute-start(bf16[2,512,128]{2,1,0:T(8,128)(2,1)S(1)} %get-tuple-element.22), channel_id=1, source_target_pairs={{0,224},{8,232},{16,240},{24,248},{32,0},{40,8},{48,16},{56,24},{6... | collective-permute-start | bytes 786440 | tf_op jit(solution)/shard_map/ppermute | solution.py:316
  15.7 5.4 %collective-permute-start.2 = (bf16[2,2,128,128]{3,2,1,0:T(8,128)(2,1)S(1)}, bf16[2,2,128,128]{3,2,1,0:T(8,128)(2,1)S(1)}, u32[]{:S(2)}, u32[]{:S(2)}) collective-permute-start(bf16[2,2,128,128]{3,2,1,0:T(8,128)(2,1)S(1)} %shard_map.47.refs_0_), channel_id=1, source_target_pairs={{0,4},{1,5},{2,6},{3,7},{4,0},{5,1},{6,2},{7,3},{8,12},{9,13},{10,... | collective-permute-start | bytes 393224 | tf_op jit(solution)/shard_map/ppermute | solution.py:323
  16.3 6.2 %collective-permute-start.1 = (bf16[2,2,128,128]{3,2,1,0:T(8,128)(2,1)S(1)}, bf16[2,2,128,128]{3,2,1,0:T(8,128)(2,1)S(1)}, u32[]{:S(2)}, u32[]{:S(2)}) collective-permute-start(bf16[2,2,128,128]{3,2,1,0:T(8,128)(2,1)S(1)} %shard_map.47.refs_0_), channel_id=1, source_target_pairs={{0,2},{1,3},{2,4},{3,5},{4,6},{5,7},{6,0},{7,1},{8,10},{9,11},{10,... | collective-permute-start | bytes 393224 | tf_op jit(solution)/shard_map/ppermute | solution.py:323
  16.9 11.8 %collective-permute-start.14 = (bf16[2,512,128]{2,1,0:T(8,128)(2,1)S(1)}, bf16[2,512,128]{2,1,0:T(8,128)(2,1)S(1)}, u32[]{:S(2)}, u32[]{:S(2)}) collective-permute-start(bf16[2,512,128]{2,1,0:T(8,128)(2,1)S(1)} %collective-permute-done.11.refs_0_), channel_id=1, source_target_pairs={{0,4},{1,5},{2,6},{3,7},{4,0},{5,1},{6,2},{7,3},{8,12},{9,13},{10,... | collective-permute-start | bytes 786440 | tf_op jit(solution)/shard_map/ppermute | solution.py:323
  18.7 12.3 %collective-permute-start.13 = (bf16[2,512,128]{2,1,0:T(8,128)(2,1)S(1)}, bf16[2,512,128]{2,1,0:T(8,128)(2,1)S(1)}, u32[]{:S(2)}, u32[]{:S(2)}) collective-permute-start(bf16[2,512,128]{2,1,0:T(8,128)(2,1)S(1)} %collective-permute-done.11.refs_0_), channel_id=1, source_target_pairs={{0,6},{1,7},{2,0},{3,1},{4,2},{5,3},{6,4},{7,5},{8,14},{9,15},{10,... | collective-permute-start | bytes 786440 | tf_op jit(solution)/shard_map/ppermute | solution.py:323
  24.4 3.5 %collective-permute-start.15 = (bf16[2,128,128]{2,1,0:T(8,128)(2,1)S(1)}, bf16[2,128,128]{2,1,0:T(8,128)(2,1)S(1)}, u32[]{:S(2)}, u32[]{:S(2)}) collective-permute-start(bf16[2,128,128]{2,1,0:T(8,128)(2,1)S(1)} %get-tuple-element.24), channel_id=1, source_target_pairs={{0,224},{8,232},{16,240},{24,248},{32,0},{40,8},{48,16},{56,24},{6... | collective-permute-start | bytes 196616 | tf_op jit(solution)/shard_map/ppermute | solution.py:316
  25.4 25.8 %collective-permute-start.17 = (bf16[2,320,512]{2,1,0:T(8,128)(2,1)S(1)}, bf16[2,320,512]{2,1,0:T(8,128)(2,1)S(1)}, u32[]{:S(2)}, u32[]{:S(2)}) collective-permute-start(bf16[2,320,512]{2,1,0:T(8,128)(2,1)S(1)} %get-tuple-element.19.upper), channel_id=1, source_target_pairs={{0,240},{8,248},{16,0},{24,8},{32,16},{40,24},{48,32},{56,40},{64,... | collective-permute-start | bytes 1966088 | tf_op jit(solution)/shard_map/ppermute | solution.py:316
  26.9 11.1 %collective-permute-start.12 = (bf16[2,512,128]{2,1,0:T(8,128)(2,1)S(1)}, bf16[2,512,128]{2,1,0:T(8,128)(2,1)S(1)}, u32[]{:S(2)}, u32[]{:S(2)}) collective-permute-start(bf16[2,512,128]{2,1,0:T(8,128)(2,1)S(1)} %collective-permute-done.11.refs_0_), channel_id=1, source_target_pairs={{0,2},{1,3},{2,4},{3,5},{4,6},{5,7},{6,0},{7,1},{8,10},{9,11},{10,... | collective-permute-start | bytes 786440 | tf_op jit(solution)/shard_map/ppermute | solution.py:323
  27.8 16.4 %collective-permute-start.10 = (bf16[2,512,128]{2,1,0:T(8,128)(2,1)S(1)}, bf16[2,512,128]{2,1,0:T(8,128)(2,1)S(1)}, u32[]{:S(2)}, u32[]{:S(2)}) collective-permute-start(bf16[2,512,128]{2,1,0:T(8,128)(2,1)S(1)} %collective-permute-done.7.refs_0_), channel_id=1, source_target_pairs={{0,4},{1,5},{2,6},{3,7},{4,0},{5,1},{6,2},{7,3},{8,12},{9,13},{10,... | collective-permute-start | bytes 786440 | tf_op jit(solution)/shard_map/ppermute | solution.py:323
  28.7 15.6 %collective-permute-start.9 = (bf16[2,512,128]{2,1,0:T(8,128)(2,1)S(1)}, bf16[2,512,128]{2,1,0:T(8,128)(2,1)S(1)}, u32[]{:S(2)}, u32[]{:S(2)}) collective-permute-start(bf16[2,512,128]{2,1,0:T(8,128)(2,1)S(1)} %collective-permute-done.7.refs_0_), channel_id=1, source_target_pairs={{0,6},{1,7},{2,0},{3,1},{4,2},{5,3},{6,4},{7,5},{8,14},{9,15},{10,... | collective-permute-start | bytes 786440 | tf_op jit(solution)/shard_map/ppermute | solution.py:323
  31.0 13.2 %collective-permute-start.8 = (bf16[2,512,128]{2,1,0:T(8,128)(2,1)S(1)}, bf16[2,512,128]{2,1,0:T(8,128)(2,1)S(1)}, u32[]{:S(2)}, u32[]{:S(2)}) collective-permute-start(bf16[2,512,128]{2,1,0:T(8,128)(2,1)S(1)} %collective-permute-done.7.refs_0_), channel_id=1, source_target_pairs={{0,2},{1,3},{2,4},{3,5},{4,6},{5,7},{6,0},{7,1},{8,10},{9,11},{10,... | collective-permute-start | bytes 786440 | tf_op jit(solution)/shard_map/ppermute | solution.py:323
  38.0 31.4 %collective-permute-start.6 = (bf16[2,512,512]{2,1,0:T(8,128)(2,1)S(1)}, bf16[2,512,512]{2,1,0:T(8,128)(2,1)S(1)}, u32[]{:S(2)}, u32[]{:S(2)}) collective-permute-start(bf16[2,512,512]{2,1,0:T(8,128)(2,1)S(1)} %get-tuple-element.21), channel_id=1, source_target_pairs={{0,8},{8,0},{16,24},{24,16},{32,40},{40,32},{48,56},{56,48},{64,72... | collective-permute-start | bytes 3145736 | tf_op jit(solution)/shard_map/ppermute | solution.py:319
  45.5 23.9 %collective-permute-start.16 = (bf16[2,512,512]{2,1,0:T(8,128)(2,1)S(1)}, bf16[2,512,512]{2,1,0:T(8,128)(2,1)S(1)}, u32[]{:S(2)}, u32[]{:S(2)}) collective-permute-start(bf16[2,512,512]{2,1,0:T(8,128)(2,1)S(1)} %shard_map.53.refs_0_), channel_id=1, source_target_pairs={{0,8},{8,0},{16,24},{24,16},{32,40},{40,32},{48,56},{56,48},{64,72... | collective-permute-start | bytes 3145736 | tf_op jit(solution)/shard_map/ppermute | solution.py:319
  51.2 15.5 %collective-permute-start.18 = (bf16[2,320,512]{2,1,0:T(8,128)(2,1)S(1)}, bf16[2,320,512]{2,1,0:T(8,128)(2,1)S(1)}, u32[]{:S(2)}, u32[]{:S(2)}) collective-permute-start(bf16[2,320,512]{2,1,0:T(8,128)(2,1)S(1)} %collective-permute-done.17.refs_0_), channel_id=1, source_target_pairs={{0,8},{8,0},{16,24},{24,16},{32,40},{40,32},{48,56},{56,48},{64,72... | collective-permute-start | bytes 1966088 | tf_op jit(solution)/shard_map/ppermute | solution.py:319
  51.3 10.3 %collective-permute-start.4 = (bf16[2,192,512]{2,1,0:T(8,128)(2,1)S(1)}, bf16[2,192,512]{2,1,0:T(8,128)(2,1)S(1)}, u32[]{:S(2)}, u32[]{:S(2)}) collective-permute-start(bf16[2,192,512]{2,1,0:T(8,128)(2,1)S(1)} %get-tuple-element.20), channel_id=1, source_target_pairs={{0,240},{8,248},{16,0},{24,8},{32,16},{40,24},{48,32},{56,40},{64,... | collective-permute-start | bytes 1179656 | tf_op jit(solution)/shard_map/ppermute | solution.py:316
  61.6 10.4 %collective-permute-start.5 = (bf16[2,192,512]{2,1,0:T(8,128)(2,1)S(1)}, bf16[2,192,512]{2,1,0:T(8,128)(2,1)S(1)}, u32[]{:S(2)}, u32[]{:S(2)}) collective-permute-start(bf16[2,192,512]{2,1,0:T(8,128)(2,1)S(1)} %collective-permute-done.4.refs_2_), channel_id=1, source_target_pairs={{0,8},{8,0},{16,24},{24,16},{32,40},{40,32},{48,56},{56,48},{64,72... | collective-permute-start | bytes 1179656 | tf_op jit(solution)/shard_map/ppermute | solution.py:319
